TPU v7x, 32 devices: a whole 2x2x4 slice. The times are simulated.
32 devices in a mesh: pp: 2 (over core), ep: 16 (over z, y, x), tp: 1.
Axes of the slice: x: 2, y: 2, z: 4, core: 2. Of those that a mesh axis runs over, the one named last changes fastest.
Arguments:
- acts: bfloat16 [2, 96, 3072], P(None, 'ep'), may hold values from -6 to 6
- route_ids: int32 [2, 2, 96, 8], P('pp', None, 'ep'), may hold values from 0 to 23, all different within a row; in each aligned block of 6 rows (0 to 5, 6 to 11, ..., all dimensions but the last counted through in order) at most 2 rows name the same one
- norm_gain: bfloat16 [2, 3072], P('pp'), may hold values from 0.5 to 1.5
- router: bfloat16 [2, 3072, 24], P('pp'), may hold values from -0.109375 to 0.109375
- dense_gate: bfloat16 [2, 3072, 6144], P('pp', None, ('ep', 'tp')), may hold values from -0.109375 to 0.109375
- dense_up: bfloat16 [2, 3072, 6144], P('pp', None, ('ep', 'tp')), may hold values from -0.109375 to 0.109375
- dense_down: bfloat16 [2, 6144, 3072], P('pp', ('ep', 'tp')), may hold values from -0.078125 to 0.078125
- expert_gate: bfloat16 [2, 16, 3072, 1024], P('pp', 'ep', None, 'tp'), may hold values from -0.109375 to 0.109375
- expert_up: bfloat16 [2, 16, 3072, 1024], P('pp', 'ep', None, 'tp'), may hold values from -0.109375 to 0.109375
- expert_down: bfloat16 [2, 16, 1024, 3072], P('pp', 'ep', 'tp'), may hold values from -0.1875 to 0.1875
Outputs:
- layer_out: bfloat16 [2, 2, 96, 3072], P('pp', None, 'ep')
Inputs may be any that keep to these rules, and one draw needn't show every extreme that they name: `route_ids`: the 8 ids of a token differ. In each layer and microbatch, among the 6 tokens of one ep index no id is named by more than 2 tokens, a bound that some block reaches.
All inputs are finite; a program needn't handle non-finite values.
Results may differ from a plain program's by a relative error of at most 0.008.
Values may be sent and summed in bfloat16 or wider, within the bound.
No kernel may reach another device: no remote copies, remote signals or barrier semaphores. Data moves between devices by JAX's collectives and lax.ppermute only.
A program may use at most 128 MiB of HBM per device.

v0:
```python
import jax
import jax.numpy as jnp
from jax import lax
from jax.sharding import PartitionSpec as P


def from_behind(block, axis, distance):
    devices = range(lax.axis_size(axis))
    route = [(i - distance, i) for i in devices if i - distance in devices]
    return lax.ppermute(block, axis, route)


def normalize(inputs, gain):
    widened = inputs.astype(jnp.float32)
    spread = jnp.mean(widened * widened, axis=-1, keepdims=True)
    normed = (widened * lax.rsqrt(spread + 1e-06) * gain.astype(jnp.float32)).astype(jnp.bfloat16)
    return (widened, normed)


def gated_block(inputs, w_gate, w_up, w_down):
    gate_part = jnp.dot(inputs, w_gate, preferred_element_type=jnp.float32)
    up_part = jnp.dot(inputs, w_up, preferred_element_type=jnp.float32)
    hidden = (jax.nn.silu(gate_part) * up_part).astype(jnp.bfloat16)
    return jnp.dot(hidden, w_down, preferred_element_type=jnp.float32)


def choice_weights(normed, route_rows, router_w, n_real):
    n_total = router_w.shape[1]
    gates = jax.nn.sigmoid(jnp.dot(normed, router_w, preferred_element_type=jnp.float32))
    picked = (route_rows[:, :, None] == jnp.arange(n_total, dtype=jnp.int32)[None, None, :]).astype(
        jnp.float32
    )
    weights = jnp.sum(picked * gates[:, None, :], axis=-1)
    zero_share = jnp.sum(jnp.where(route_rows >= n_real, weights, jnp.float32(0.0)), axis=-1)
    return (weights, picked, zero_share)


def on_device(
    acts,
    route_ids,
    norm_gain,
    router,
    dense_gate,
    dense_up,
    dense_down,
    expert_gate,
    expert_up,
    expert_down,
):
    n_micro, per_group, width = acts.shape
    top_count = route_ids.shape[-1]
    n_groups = lax.axis_size("ep")
    n_pairs = lax.axis_size("tp")
    section = lax.axis_index("pp")
    group_pos = lax.axis_index("ep")
    pair_pos = lax.axis_index("tp")
    micro_rows = per_group * n_groups
    share = per_group // n_pairs
    gain = norm_gain[0]
    router_w = router[0]
    total_ids = router_w.shape[1]
    slot_count = max(2, (per_group * top_count + total_ids - 1) // total_ids)
    d_gate = dense_gate[0]
    d_up = dense_up[0]
    d_down = dense_down[0]
    e_gate = expert_gate[0, 0]
    e_up = expert_up[0, 0]
    e_down = expert_down[0, 0]
    slot_range = jnp.arange(slot_count, dtype=jnp.float32)
    incoming = jnp.zeros((per_group, width), jnp.bfloat16)
    outputs = jnp.zeros((n_micro, per_group, width), jnp.bfloat16)
    for tick_index in range(n_micro + 1):
        local_micro = tick_index - section
        micro_index = jnp.clip(local_micro, 0, n_micro - 1)
        valid = jnp.logical_and(local_micro >= 0, local_micro < n_micro)
        first_input = acts[min(tick_index, n_micro - 1)]
        current = jnp.where(section == 0, first_input, incoming)
        route_rows = lax.dynamic_index_in_dim(route_ids[0], micro_index, 0, keepdims=False)
        widened, normed = normalize(current, gain)
        weights, picked, zero_share = choice_weights(normed, route_rows, router_w, n_groups)
        all_normed = lax.all_gather(normed, "ep", axis=0, tiled=True)
        real_pick = picked[:, :, :n_groups]
        hot = jnp.sum(real_pick, axis=1)
        coef = jnp.einsum("tk,tke->te", weights, real_pick, precision=lax.Precision.HIGHEST)
        position = jnp.cumsum(hot, axis=0) - hot
        select = hot.T[:, None, :] * (position.T[:, None, :] == slot_range[None, :, None]).astype(
            jnp.float32
        )
        outgoing = jnp.einsum(
            "esi,id->esd", select.astype(jnp.bfloat16), normed, preferred_element_type=jnp.float32
        ).astype(jnp.bfloat16)
        received = lax.all_to_all(outgoing, "ep", split_axis=0, concat_axis=0, tiled=True)
        flat = received.reshape(-1, width)
        produced = gated_block(flat, e_gate, e_up, e_down).reshape(received.shape[:-1] + (width,))
        returned = lax.all_to_all(produced, "ep", split_axis=0, concat_axis=0, tiled=True)
        own_rows = jnp.einsum(
            "esi,esd->id", select * coef.T[:, None, :], returned, precision=lax.Precision.HIGHEST
        )
        extra = lax.dynamic_update_slice_in_dim(
            jnp.zeros((micro_rows, width), jnp.float32), own_rows, group_pos * per_group, 0
        )
        summed = lax.psum_scatter(
            gated_block(all_normed, d_gate, d_up, d_down) + extra,
            ("ep", "tp"),
            scatter_dimension=0,
            tiled=True,
        )
        offset = pair_pos * share
        own_inputs = lax.dynamic_slice_in_dim(widened, offset, share, 0)
        own_normed = lax.dynamic_slice_in_dim(normed, offset, share, 0).astype(jnp.float32)
        own_zero = lax.dynamic_slice_in_dim(zero_share, offset, share, 0)
        result_part = (own_inputs + summed + own_zero[:, None] * own_normed).astype(jnp.bfloat16)
        finished = lax.all_gather(result_part, "tp", axis=0, tiled=True)
        updated = lax.dynamic_update_index_in_dim(outputs, finished, micro_index, 0)
        outputs = jnp.where(valid, updated, outputs)
        if tick_index < n_micro:
            incoming = from_behind(finished, "pp", 1)
    return outputs[None]


def solution(mesh):
    return jax.shard_map(
        on_device,
        mesh=mesh,
        in_specs=(
            P(None, "ep", None),
            P("pp", None, "ep", None),
            P("pp", None),
            P("pp", None, None),
            P("pp", None, ("ep", "tp")),
            P("pp", None, ("ep", "tp")),
            P("pp", ("ep", "tp"), None),
            P("pp", "ep", None, "tp"),
            P("pp", "ep", None, "tp"),
            P("pp", "ep", "tp", None),
        ),
        out_specs=P("pp", None, "ep", None),
        check_vma=False,
    )
```

profile of v0, /device:TPU:0, one launch (start us, length us, event | category | flops | bytes accessed | tf_op | source)
XLA Modules:
  0.0 461.7 jit_solution(911177788010176452)
XLA Ops:
  1.0 1.7 fusion.201
  4.8 8.3 %all-to-all-start = ((bf16[16,2,3072]{2,1,0:T(2,128)(2,1)}), bf16[16,2,3072]{2,1,0:T(2,128)(2,1)S(1)}, u32[]{:S(2)}, u32[]{:S(2)}) async-start(bf16[16,2,3072]{2,1,0:T(2,128)(2,1)} %copy.46), calls=%async_computation | async-start | bytes 393216 | tf_op jit(solution)/shard_map/all_to_all | solution.py:92
  15.1 48.1 %all-gather = bf16[16,6,3072]{2,1,0:T(8,128)(2,1)} all-gather(bf16[1,6,3072]{2,1,0:T(8,128)(2,1)S(1)} %fusion.192), channel_id=1, replica_groups=mesh['pp'=2,'ep'=16,'tp'=1] {'ep'}, dimensions={0}, use_global_device_ids=true | all-gather | bytes 626688 | tf_op jit(solution)/shard_map/all_gather | solution.py:81
  63.3 4.1 fusion.19
  69.2 4.0 fusion.7
  74.2 3.6 all-to-all-start.1
  81.0 2.9 fusion.40
  83.9 3.8 fusion.28
  87.7 1.4 fusion.23
  89.1 1.6 add.116
  90.7 50.0 %fusion = f32[8,3072]{1,0:T(8,128)S(1)} fusion(f32[96,3072]{1,0:T(8,128)} %add.116), kind=kCustom, calls=%all-reduce-scatter | all-reduce-scatter fusion | flops 393217 | bytes 1278464
  140.7 1.8 collective-permute-start.2
  143.8 5.1 %collective-permute-start.4 = (f32[8,3072]{1,0:T(8,128)S(1)}, f32[8,3072]{1,0:T(8,128)S(1)}, u32[]{:S(2)}, u32[]{:S(2)}) collective-permute-start(f32[8,3072]{1,0:T(8,128)S(1)} %fusion), channel_id=1, source_target_pairs={{0,3},{1,4},{2,5},{3,6},{4,7},{5,8},{6,9},{7,10},{8,11},{9,12},{10... | collective-permute-start | bytes 294920
  148.9 3.3 collective-permute-start.5
  152.9 1.4 collective-permute-done.5
  161.3 4.7 %all-to-all-start.2 = ((bf16[16,2,3072]{2,1,0:T(2,128)(2,1)}), bf16[16,2,3072]{2,1,0:T(2,128)(2,1)S(1)}, u32[]{:S(2)}, u32[]{:S(2)}) async-start(bf16[16,2,3072]{2,1,0:T(2,128)(2,1)} %copy.52), calls=%async_computation.2 | async-start | bytes 393216 | tf_op jit(solution)/shard_map/all_to_all | solution.py:92
  166.1 48.3 %all-gather.1 = bf16[16,6,3072]{2,1,0:T(8,128)(2,1)} all-gather(bf16[1,6,3072]{2,1,0:T(8,128)(2,1)S(1)} %fusion.198), channel_id=1, replica_groups=mesh['pp'=2,'ep'=16,'tp'=1] {'ep'}, dimensions={0}, use_global_device_ids=true | all-gather | bytes 626688 | tf_op jit(solution)/shard_map/all_gather | solution.py:81
  214.5 4.0 fusion.17
  218.5 4.0 fusion.72
  222.5 4.0 fusion.5
  227.5 3.7 all-to-all-start.3
  231.4 1.3 reshape.96
  232.8 2.8 fusion.38
  235.6 3.8 fusion.26
  239.5 1.4 all-to-all-done.3
  240.9 1.3 fusion.22
  242.2 1.6 add.123
  243.9 49.4 %fusion.1 = f32[8,3072]{1,0:T(8,128)S(1)} fusion(f32[96,3072]{1,0:T(8,128)} %add.123), kind=kCustom, calls=%all-reduce-scatter.1 | all-reduce-scatter fusion | flops 393217 | bytes 1278464
  295.9 4.6 collective-permute-start.8
  300.5 2.8 collective-permute-start.9
  303.4 2.1 collective-permute-done.9
  306.1 2.4 concatenate.1
  313.3 5.3 %all-to-all-start.4 = ((bf16[16,2,3072]{2,1,0:T(2,128)(2,1)}), bf16[16,2,3072]{2,1,0:T(2,128)(2,1)S(1)}, u32[]{:S(2)}, u32[]{:S(2)}) async-start(bf16[16,2,3072]{2,1,0:T(2,128)(2,1)} %copy.57), calls=%async_computation.4 | async-start | bytes 393216 | tf_op jit(solution)/shard_map/all_to_all | solution.py:92
  318.8 48.3 %all-gather.2 = bf16[16,6,3072]{2,1,0:T(8,128)(2,1)} all-gather(bf16[1,6,3072]{2,1,0:T(8,128)(2,1)S(1)} %fusion.195), channel_id=1, replica_groups=mesh['pp'=2,'ep'=16,'tp'=1] {'ep'}, dimensions={0}, use_global_device_ids=true | all-gather | bytes 626688 | tf_op jit(solution)/shard_map/all_gather | solution.py:81
  367.1 4.0 fusion.15
  371.1 4.0 fusion.69
  375.1 4.0 fusion.3
  380.2 3.6 all-to-all-start.5
  385.2 2.9 fusion.36
  388.1 3.8 fusion.24
  391.9 1.4 all-to-all-done.5
  393.3 1.3 fusion.21
  394.7 1.6 add.130
  396.3 49.4 %fusion.2 = f32[8,3072]{1,0:T(8,128)S(1)} fusion(f32[96,3072]{1,0:T(8,128)} %add.130), kind=kCustom, calls=%all-reduce-scatter.2 | all-reduce-scatter fusion | flops 393217 | bytes 1278464
  448.3 4.6 collective-permute-start.12
  452.9 2.7 collective-permute-start.13
  455.8 2.1 collective-permute-done.13
  458.5 2.4 concatenate.2
  (117 shorter events, 36.1 us)
Async XLA Ops:
  0.0 83.9 %copy-start = (bf16[1,384,3072]{2,1,0:T(8,128)(2,1)S(1)}, bf16[1,384,3072]{2,1,0:T(8,128)(2,1)}, u32[]{:S(2)}) copy-start(bf16[1,384,3072]{2,1,0:T(8,128)(2,1)} %param.16) | copy-start | bytes 7077892
  2.9 10.3 %copy-start.9 = (f32[6]{0:T(128)}, f32[6]{0:T(128)S(1)}, u32[]{:S(2)}) copy-start(f32[6]{0:T(128)S(1)} %add_rsqrt_fusion.2) | copy-start | bytes 76
  4.8 58.4 %all-to-all-start = ((bf16[16,2,3072]{2,1,0:T(2,128)(2,1)}), bf16[16,2,3072]{2,1,0:T(2,128)(2,1)S(1)}, u32[]{:S(2)}, u32[]{:S(2)}) async-start(bf16[16,2,3072]{2,1,0:T(2,128)(2,1)} %copy.46), calls=%async_computation | async-start | bytes 393216 | tf_op jit(solution)/shard_map/all_to_all | solution.py:92
  14.5 0.6 copy-start.6
  63.3 4.6 copy-start.1
  73.1 6.7 %copy-start.12 = (u32[32]{0:T(128)S(1)}, u32[32]{0:T(128)}, u32[]{:S(2)}) copy-start(u32[32]{0:T(128)} %constant.91) | copy-start | bytes 388
  74.2 13.5 %all-to-all-start.1 = ((f32[16,2,3072]{2,1,0:T(2,128)}), f32[16,2,3072]{2,1,0:T(2,128)S(1)}, u32[]{:S(2)}, u32[]{:S(2)}) async-start(f32[16,2,3072]{2,1,0:T(2,128)} %copy.48), calls=%async_computation.1 | async-start | bytes 786432 | tf_op jit(solution)/shard_map/all_to_all | solution.py:95
  140.7 13.7 %collective-permute-start.2 = (f32[8,3072]{1,0:T(8,128)S(1)}, f32[8,3072]{1,0:T(8,128)S(1)}, u32[]{:S(2)}, u32[]{:S(2)}) collective-permute-start(f32[8,3072]{1,0:T(8,128)S(1)} %fusion), channel_id=1, source_target_pairs={{0,1},{1,2},{2,3},{3,4},{4,5},{5,6},{6,7},{7,8},{8,9},{9,10},{10,1... | collective-permute-start | bytes 294920
  142.5 11.9 %collective-permute-start.3 = (f32[8,3072]{1,0:T(8,128)S(1)}, f32[8,3072]{1,0:T(8,128)S(1)}, u32[]{:S(2)}, u32[]{:S(2)}) collective-permute-start(f32[8,3072]{1,0:T(8,128)S(1)} %fusion), channel_id=1, source_target_pairs={{0,2},{1,3},{2,4},{3,5},{4,6},{5,7},{6,8},{7,9},{8,10},{9,11},{10,... | collective-permute-start | bytes 294920
  143.8 10.6 %collective-permute-start.4 = (f32[8,3072]{1,0:T(8,128)S(1)}, f32[8,3072]{1,0:T(8,128)S(1)}, u32[]{:S(2)}, u32[]{:S(2)}) collective-permute-start(f32[8,3072]{1,0:T(8,128)S(1)} %fusion), channel_id=1, source_target_pairs={{0,3},{1,4},{2,5},{3,6},{4,7},{5,8},{6,9},{7,10},{8,11},{9,12},{10... | collective-permute-start | bytes 294920
  148.9 5.5 %collective-permute-start.5 = (f32[6,3072]{1,0:T(8,128)S(1)}, f32[6,3072]{1,0:T(8,128)S(1)}, u32[]{:S(2)}, u32[]{:S(2)}) collective-permute-start(f32[6,3072]{1,0:T(8,128)S(1)} %slice.36), channel_id=1, source_target_pairs={{0,4},{1,5},{2,6},{3,7},{4,8},{5,9},{6,10},{7,11},{8,12},{9,13},{1... | collective-permute-start | bytes 221192
  155.7 2.2 collective-permute-start
  158.9 2.4 copy-start.10
  161.3 53.1 %all-to-all-start.2 = ((bf16[16,2,3072]{2,1,0:T(2,128)(2,1)}), bf16[16,2,3072]{2,1,0:T(2,128)(2,1)S(1)}, u32[]{:S(2)}, u32[]{:S(2)}) async-start(bf16[16,2,3072]{2,1,0:T(2,128)(2,1)} %copy.52), calls=%async_computation.2 | async-start | bytes 393216 | tf_op jit(solution)/shard_map/all_to_all | solution.py:92
  166.1 65.1 %copy-start.7 = (f32[6,8]{1,0:T(8,128)}, f32[6,8]{1,0:T(8,128)S(1)}, u32[]{:S(2)}) copy-start(f32[6,8]{1,0:T(8,128)S(1)} %select_reduce_fusion.1) | copy-start | bytes 580
  227.5 13.3 %all-to-all-start.3 = ((f32[16,2,3072]{2,1,0:T(2,128)}), f32[16,2,3072]{2,1,0:T(2,128)S(1)}, u32[]{:S(2)}, u32[]{:S(2)}) async-start(f32[16,2,3072]{2,1,0:T(2,128)} %copy.54), calls=%async_computation.3 | async-start | bytes 786432 | tf_op jit(solution)/shard_map/all_to_all | solution.py:95
  235.6 67.6 %copy-start.8 = (f32[6,8]{1,0:T(8,128)S(1)}, f32[6,8]{1,0:T(8,128)}, u32[]{:S(2)}) copy-start(f32[6,8]{1,0:T(8,128)} %copy-done.7) | copy-start | bytes 580
  239.5 69.0 %copy-start.11 = (f32[6]{0:T(128)S(1)}, f32[6]{0:T(128)}, u32[]{:S(2)}) copy-start(f32[6]{0:T(128)} %copy-done.10) | copy-start | bytes 76
  242.2 68.5 %copy-start.2 = (bf16[1,6,3072]{2,0,1:T(2,128)(2,1)S(1)}, bf16[1,6,3072]{2,0,1:T(2,128)(2,1)}, u32[]{:S(2)}) copy-start(bf16[1,6,3072]{2,0,1:T(2,128)(2,1)} %get-tuple-element.15) | copy-start | bytes 110596
  293.3 12.2 %collective-permute-start.6 = (f32[8,3072]{1,0:T(8,128)S(1)}, f32[8,3072]{1,0:T(8,128)S(1)}, u32[]{:S(2)}, u32[]{:S(2)}) collective-permute-start(f32[8,3072]{1,0:T(8,128)S(1)} %fusion.1), channel_id=1, source_target_pairs={{0,1},{1,2},{2,3},{3,4},{4,5},{5,6},{6,7},{7,8},{8,9},{9,10},{10,1... | collective-permute-start | bytes 294920
  294.6 10.9 %collective-permute-start.7 = (f32[8,3072]{1,0:T(8,128)S(1)}, f32[8,3072]{1,0:T(8,128)S(1)}, u32[]{:S(2)}, u32[]{:S(2)}) collective-permute-start(f32[8,3072]{1,0:T(8,128)S(1)} %fusion.1), channel_id=1, source_target_pairs={{0,2},{1,3},{2,4},{3,5},{4,6},{5,7},{6,8},{7,9},{8,10},{9,11},{10,... | collective-permute-start | bytes 294920
  295.9 10.2 %collective-permute-start.8 = (f32[8,3072]{1,0:T(8,128)S(1)}, f32[8,3072]{1,0:T(8,128)}, u32[]{:S(2)}, u32[]{:S(2)}) collective-permute-start(f32[8,3072]{1,0:T(8,128)S(1)} %fusion.1), channel_id=1, source_target_pairs={{0,3},{1,4},{2,5},{3,6},{4,7},{5,8},{6,9},{7,10},{8,11},{9,12},{10... | collective-permute-start | bytes 294920
  300.5 5.0 %collective-permute-start.9 = (f32[6,3072]{1,0:T(8,128)S(1)}, f32[6,3072]{1,0:T(8,128)S(1)}, u32[]{:S(2)}, u32[]{:S(2)}) collective-permute-start(f32[6,3072]{1,0:T(8,128)S(1)} %slice.37), channel_id=1, source_target_pairs={{0,4},{1,5},{2,6},{3,7},{4,8},{5,9},{6,10},{7,11},{8,12},{9,13},{1... | collective-permute-start | bytes 221192
  305.4 0.6 copy-start.4
  308.6 2.2 collective-permute-start.1
  313.3 53.8 %all-to-all-start.4 = ((bf16[16,2,3072]{2,1,0:T(2,128)(2,1)}), bf16[16,2,3072]{2,1,0:T(2,128)(2,1)S(1)}, u32[]{:S(2)}, u32[]{:S(2)}) async-start(bf16[16,2,3072]{2,1,0:T(2,128)(2,1)} %copy.57), calls=%async_computation.4 | async-start | bytes 393216 | tf_op jit(solution)/shard_map/all_to_all | solution.py:92
  380.2 13.2 %all-to-all-start.5 = ((f32[16,2,3072]{2,1,0:T(2,128)}), f32[16,2,3072]{2,1,0:T(2,128)S(1)}, u32[]{:S(2)}, u32[]{:S(2)}) async-start(f32[16,2,3072]{2,1,0:T(2,128)} %copy.59), calls=%async_computation.5 | async-start | bytes 786432 | tf_op jit(solution)/shard_map/all_to_all | solution.py:95
  394.7 66.2 %copy-start.3 = (bf16[1,2,6,3072]{3,2,1,0:T(8,128)(2,1)S(1)}, bf16[1,2,6,3072]{3,2,1,0:T(8,128)(2,1)}, u32[]{:S(2)}) copy-start(bf16[1,2,6,3072]{3,2,1,0:T(8,128)(2,1)} %copy.121) | copy-start | bytes 221188
  445.7 12.1 %collective-permute-start.10 = (f32[8,3072]{1,0:T(8,128)S(1)}, f32[8,3072]{1,0:T(8,128)S(1)}, u32[]{:S(2)}, u32[]{:S(2)}) collective-permute-start(f32[8,3072]{1,0:T(8,128)S(1)} %fusion.2), channel_id=1, source_target_pairs={{0,1},{1,2},{2,3},{3,4},{4,5},{5,6},{6,7},{7,8},{8,9},{9,10},{10,1... | collective-permute-start | bytes 294920
  447.0 10.8 %collective-permute-start.11 = (f32[8,3072]{1,0:T(8,128)S(1)}, f32[8,3072]{1,0:T(8,128)S(1)}, u32[]{:S(2)}, u32[]{:S(2)}) collective-permute-start(f32[8,3072]{1,0:T(8,128)S(1)} %fusion.2), channel_id=1, source_target_pairs={{0,2},{1,3},{2,4},{3,5},{4,6},{5,7},{6,8},{7,9},{8,10},{9,11},{10,... | collective-permute-start | bytes 294920
  448.3 10.2 %collective-permute-start.12 = (f32[8,3072]{1,0:T(8,128)S(1)}, f32[8,3072]{1,0:T(8,128)}, u32[]{:S(2)}, u32[]{:S(2)}) collective-permute-start(f32[8,3072]{1,0:T(8,128)S(1)} %fusion.2), channel_id=1, source_target_pairs={{0,3},{1,4},{2,5},{3,6},{4,7},{5,8},{6,9},{7,10},{8,11},{9,12},{10... | collective-permute-start | bytes 294920
  452.9 4.9 %collective-permute-start.13 = (f32[6,3072]{1,0:T(8,128)S(1)}, f32[6,3072]{1,0:T(8,128)S(1)}, u32[]{:S(2)}, u32[]{:S(2)}) collective-permute-start(f32[6,3072]{1,0:T(8,128)S(1)} %slice.38), channel_id=1, source_target_pairs={{0,4},{1,5},{2,6},{3,7},{4,8},{5,9},{6,10},{7,11},{8,12},{9,13},{1... | collective-permute-start | bytes 221192
  457.8 0.6 copy-start.5
where the time goes:
time: 464 us; the launch traced here: 462 us
  blocking collectives  293 us (63%)
  starting transfers between devices  63.1 us (14%)
  matrix products  61.8 us (13%)
  local copies, waits for them, and re-layouts  27.9 us (6%)
  waiting for transfers between devices  9.39 us (2%)
  other arithmetic  5.04 us (1%)
    unnamed x3, blocking collectives  149 us
    all_gather x3, blocking collectives, on_device(): all_normed = lax.all_gather(normed, 'ep', axis=0, tiled=True)  145 us
    unnamed x12, starting transfers between devices  31.3 us
    dot_general x6, matrix products, gated_block(): return jnp.dot(hidden, w_down, preferred_element_type=jnp.float32)  23.4 us
    dot_general x6, matrix products, gated_block(): gate_part = jnp.dot(inputs, w_gate, preferred_element_type=jnp.float32)  20.6 us
    all_to_all x3, starting transfers between devices, on_device(): lax.all_to_all(outgoing, 'ep', split_axis=0, concat_axis=0, tiled=True)  18.3 us
    unnamed x38, local copies, waits for them, and re-layouts  12.9 us
    all_to_all x3, starting transfers between devices, on_device(): lax.all_to_all(produced, 'ep', split_axis=0, concat_axis=0, tiled=True)  10.8 us
  transfers between devices with their start and end apart: 20, of which 7 were waited for; matrix products, arithmetic and copies ran while one was open for 6% of the time, Pallas kernels for 0%

commit v1 on v0

v1 whole, which is shorter than its diff:
```python
import jax
import jax.numpy as jnp
from jax import lax
from jax.sharding import PartitionSpec as P


def exchange(blocks, axes):
    return lax.all_to_all(blocks, axes, split_axis=0, concat_axis=0, tiled=True)


def normalize(inputs, gain):
    widened = inputs.astype(jnp.float32)
    spread = jnp.mean(widened * widened, axis=-1, keepdims=True)
    normed = (widened * lax.rsqrt(spread + 1e-06) * gain.astype(jnp.float32)).astype(jnp.bfloat16)
    return (widened, normed)


def gated_block(inputs, w_gate, w_up, w_down):
    gate_part = jnp.dot(inputs, w_gate, preferred_element_type=jnp.float32)
    up_part = jnp.dot(inputs, w_up, preferred_element_type=jnp.float32)
    hidden = (jax.nn.silu(gate_part) * up_part).astype(jnp.bfloat16)
    return jnp.dot(hidden, w_down, preferred_element_type=jnp.float32)


def layer(inputs, ids, gain, router_w, dense, expert):
    rows, width = inputs.shape
    top_count = ids.shape[-1]
    n_groups = lax.axis_size("ep")
    n_pairs = lax.axis_size("tp")
    group_pos = lax.axis_index("ep")
    share = rows // n_pairs

    packed = jnp.concatenate([inputs, jnp.pad(ids, ((0, 0), (0, 128 - top_count))).astype(jnp.bfloat16)], axis=1)
    gathered = exchange(jnp.broadcast_to(packed[None], (n_groups, rows, width + 128)), "ep")
    gathered = gathered.reshape(n_groups * rows, width + 128)
    all_ids = gathered[:, width : width + top_count].astype(jnp.int32)
    _, all_normed = normalize(gathered[:, :width], gain)
    named = jnp.sum((all_ids == group_pos).astype(jnp.float32), axis=-1, keepdims=True)
    column = lax.dynamic_slice_in_dim(router_w, group_pos, 1, 1)
    gate = jax.nn.sigmoid(jnp.dot(all_normed, column, preferred_element_type=jnp.float32))
    partial = gated_block(all_normed, *dense) + (named * gate) * gated_block(all_normed, *expert)

    widened, normed = normalize(inputs, gain)
    gates = jax.nn.sigmoid(jnp.dot(normed, router_w, preferred_element_type=jnp.float32))
    id_range = jnp.arange(router_w.shape[1], dtype=jnp.int32)
    picked = jnp.sum((ids[:, :, None] == id_range[None, None, :]).astype(jnp.float32), axis=1)
    zero_share = jnp.sum(jnp.where(id_range[None, :] >= n_groups, picked * gates, 0.0), axis=-1, keepdims=True)
    base = widened + zero_share * normed.astype(jnp.float32)

    pieces = partial.astype(jnp.bfloat16).reshape(n_groups * n_pairs, share, width)
    received = exchange(pieces, ("ep", "tp"))
    own = lax.dynamic_slice_in_dim(base, lax.axis_index("tp") * share, share, 0)
    part = (own + jnp.sum(received.astype(jnp.float32), axis=0)).astype(jnp.bfloat16)
    return lax.all_gather(part, "tp", axis=0, tiled=True) if n_pairs > 1 else part


def on_device(
    acts,
    route_ids,
    norm_gain,
    router,
    dense_gate,
    dense_up,
    dense_down,
    expert_gate,
    expert_up,
    expert_down,
):
    n_micro, per_group, width = acts.shape
    n_sections = lax.axis_size("pp")
    section = lax.axis_index("pp")
    ids = route_ids[0].reshape(n_micro * per_group, -1)
    dense = (dense_gate[0], dense_up[0], dense_down[0])
    expert = (expert_gate[0, 0], expert_up[0, 0], expert_down[0, 0])

    current = acts.reshape(n_micro * per_group, width)
    result = current
    for phase in range(n_sections):
        result = lax.cond(
            section == phase,
            lambda held, fed: layer(fed, ids, norm_gain[0], router[0], dense, expert),
            lambda held, fed: held,
            result,
            current,
        )
        if phase + 1 < n_sections:
            current = lax.ppermute(result, "pp", [(phase, phase + 1)])
    return result.reshape(1, n_micro, per_group, width)


def solution(mesh):
    return jax.shard_map(
        on_device,
        mesh=mesh,
        in_specs=(
            P(None, "ep", None),
            P("pp", None, "ep", None),
            P("pp", None),
            P("pp", None, None),
            P("pp", None, ("ep", "tp")),
            P("pp", None, ("ep", "tp")),
            P("pp", ("ep", "tp"), None),
            P("pp", "ep", None, "tp"),
            P("pp", "ep", None, "tp"),
            P("pp", "ep", "tp", None),
        ),
        out_specs=P("pp", None, "ep", None),
        check_vma=False,
    )
```

time: 464 us -> 161 us (0.35)
  the two profiles are of different devices: /device:TPU:0 before, /device:TPU:1 now
where the time goes in v1:
time: 161 us; the launch traced here: 160 us
  waiting for transfers between devices  121 us (75%)
  matrix products  19.6 us (12%)
  starting transfers between devices  12.8 us (8%)
  local copies, waits for them, and re-layouts  5.65 us (4%)
    ppermute x1, waiting for transfers between devices, on_device(): current = lax.ppermute(result, 'pp', [(phase, phase + 1)])  81.2 us
    all_to_all x2, waiting for transfers between devices, exchange(): return lax.all_to_all(blocks, axes, split_axis=0, concat_axis=0, tiled=True)  39.7 us
    dot_general x2, matrix products, gated_block(): return jnp.dot(hidden, w_down, preferred_element_type=jnp.float32)  13.5 us
    all_to_all x2, starting transfers between devices, exchange(): return lax.all_to_all(blocks, axes, split_axis=0, concat_axis=0, tiled=True)  11.5 us
    dot_general x2, matrix products, gated_block(): gate_part = jnp.dot(inputs, w_gate, preferred_element_type=jnp.float32)  5.23 us
  transfers between devices with their start and end apart: 3, of which 3 were waited for; matrix products, arithmetic and copies ran while one was open for 0% of the time, Pallas kernels for 0%

profile of v1, /device:TPU:1, one launch (start us, length us, event | category | flops | bytes accessed | tf_op | source)
XLA Modules:
  0.0 160.4 jit_solution(14630249948803984350)
XLA Ops:
  0.0 0.9 copy.44
  0.9 0.8 copy.45
  1.7 0.1 reshape_squeeze.3
  1.8 1.3 collective-permute-start
  3.1 81.2 %collective-permute-done = bf16[12,3072]{1,0:T(8,128)(2,1)S(1)} collective-permute-done((bf16[12,3072]{1,0:T(8,128)(2,1)S(1)}, bf16[12,3072]{1,0:T(8,128)(2,1)S(1)}, u32[]{:S(2)}, u32[]{:S(2)}) %collective-permute-start) | collective-permute-done | bytes 73760 | tf_op jit(solution)/shard_map/ppermute | solution.py:87
  84.3 75.4 %conditional.3 = (bf16[12,3072]{1,0:T(8,128)(2,1)S(1)}) conditional(s32[]{:T(128)} %convert_element_type.92, bf16[12,3072]{1,0:T(8,128)(2,1)S(1)} %get-tuple-element.173, (bf16[12,3072]{1,0:T(8,128)(2,1)S(1)}, s32[1,2,6,8]{3,1,2,0:T(2,128)}, bf16[1,3072]{1,0:T(2,128)(2,1)}, bf16[1,3072,24]{1,2,0:T(8,128)(2,1)}, s32[12,8]{0,1:T(8,128)S(1)}, ...), branch_computations={%region_8.9_spmd, %region_9.16_spmd} | conditional | flops 5004721152 | bytes 68315888 | solution.py:79
  84.3 0.1 copy.49
  84.4 0.0 copy-start.3
  84.4 1.3 broadcast_in_dim.35
  85.7 5.7 %all-to-all-start.2 = ((bf16[16,12,3200]{2,1,0:T(8,128)(2,1)}), bf16[16,12,3200]{2,1,0:T(8,128)(2,1)S(1)}, u32[]{:S(2)}, u32[]{:S(2)}) async-start(bf16[16,12,3200]{2,1,0:T(8,128)(2,1)} %broadcast_in_dim.35), calls=%async_computation.2 | async-start | bytes 3276800 | tf_op jit(solution)/shard_map/cond/branch_1_fun/all_to_all | solution.py:8
  91.4 0.0 copy-done.3
  91.4 20.4 %all-to-all-done.2 = bf16[16,12,3200]{2,1,0:T(8,128)(2,1)S(1)} async-done(((bf16[16,12,3200]{2,1,0:T(8,128)(2,1)}), bf16[16,12,3200]{2,1,0:T(8,128)(2,1)S(1)}, u32[]{:S(2)}, u32[]{:S(2)}) %all-to-all-start.2) | async-done | bytes 1228832 | tf_op jit(solution)/shard_map/cond/branch_1_fun/all_to_all | solution.py:8
  111.9 0.3 reshape.92
  112.2 0.3 fusion.45
  112.5 0.1 copy.56
  112.6 0.0 copy-start.5
  112.6 4.4 %fusion.81 = f32[192,1024]{1,0:T(8,128)S(1)} fusion(bf16[3072,1024]{1,0:T(8,128)(2,1)} %get-tuple-element.78, f32[3072]{0:T(1024)S(1)} %bitcast.47, f32[192]{0:T(256)S(1)} %add_rsqrt_fusion.2, bf16[192,3200]{1,0:T(8,128)(2,1)S(1)} %reshape.92), kind=kOutput, calls=%fused_computation.110 | convolution fusion | flops 1210318848 | bytes 8270848 | tf_op jit(solution)/shard_map/cond/branch_1_fun/dot_general | solution.py:19
  117.0 0.0 copy-done.5
  117.0 0.0 copy-start.7
  117.0 0.9 fusion.86
  117.9 0.0 copy-done.7
  117.9 0.5 fusion.73
  118.4 8.9 %convolution_multiply_fusion.3 = f32[192,3072]{1,0:T(8,128)} fusion(bf16[1024,3072]{1,0:T(8,128)(2,1)} %get-tuple-element.80, f32[192]{0:T(256)S(1)} %divide_multiply_fusion.1, bf16[3072,1024]{1,0:T(8,128)(2,1)} %get-tuple-element.79, f32[192,1024]{1,0:T(8,128)S(1)} %fusion.81, f32[3072]{0:T(1024)S(1)} %bitcast.50, f32[192]{0:T(256)S(1)} %add_rsqrt_fusion.2, ...), kind=kOutput, calls=%fused_computation.57 | convolution fusion | flops 2420047872 | bytes 16922624 | tf_op jit(solution)/shard_map/cond/branch_1_fun/dot_general | solution.py:22
  127.3 4.6 %fusion.44 = bf16[192,3072]{1,0:T(8,128)(2,1)S(1)} fusion(f32[192,3072]{1,0:T(8,128)} %convolution_multiply_fusion.3, bf16[384,3072]{1,0:T(8,128)(2,1)} %get-tuple-element.77, bf16[3072,384]{1,0:T(8,128)(2,1)} %get-tuple-element.76, f32[192,384]{1,0:T(8,128)S(1)} %fusion.86, f32[3072]{0:T(1024)S(1)} %bitcast.51, f32[192]{0:T(256)S(1)} %add_rsqrt_fusion.2, ...), kind=kOutput, calls=%fused_computation.58 | convolution fusion | flops 909950976 | bytes 9745408 | tf_op jit(solution)/shard_map/cond/branch_1_fun/dot_general | solution.py:22
  131.9 0.0 copy-start.1
  131.9 1.3 reshape.94
  133.3 5.8 %all-to-all-start.3 = ((bf16[16,12,3072]{2,1,0:T(8,128)(2,1)}), bf16[16,12,3072]{2,1,0:T(8,128)(2,1)S(1)}, u32[]{:S(2)}, u32[]{:S(2)}) async-start(bf16[16,12,3072]{2,1,0:T(8,128)(2,1)} %reshape.94), calls=%async_computation.3 | async-start | bytes 3145728 | tf_op jit(solution)/shard_map/cond/branch_1_fun/all_to_all | solution.py:8
  139.1 0.0 copy-done.1
  139.1 0.1 convert_reduce_fusion.4
  139.2 0.1 fusion.63
  139.4 0.4 fusion.55
  139.7 19.3 %all-to-all-done.3 = bf16[16,12,3072]{2,1,0:T(8,128)(2,1)S(1)} async-done(((bf16[16,12,3072]{2,1,0:T(8,128)(2,1)}), bf16[16,12,3072]{2,1,0:T(8,128)(2,1)S(1)}, u32[]{:S(2)}, u32[]{:S(2)}) %all-to-all-start.3) | async-done | bytes 1179680 | tf_op jit(solution)/shard_map/cond/branch_1_fun/all_to_all | solution.py:8
  159.0 0.3 convert_reduce_fusion.3
  159.3 0.1 fusion.67
  159.7 0.7 copy.50
  (14 shorter events, 0.2 us)
Async XLA Ops:
  1.8 82.5 %collective-permute-start = (bf16[12,3072]{1,0:T(8,128)(2,1)S(1)}, bf16[12,3072]{1,0:T(8,128)(2,1)S(1)}, u32[]{:S(2)}, u32[]{:S(2)}) collective-permute-start(bf16[12,3072]{1,0:T(8,128)(2,1)S(1)} %get-tuple-element.173), channel_id=1, source_target_pairs={{0,16},{1,17},{2,18},{3,19},{4,20},{5,21},{6,22},{7,23},{8,24},{9,... | collective-permute-start | bytes 221192 | tf_op jit(solution)/shard_map/ppermute | solution.py:87
  84.4 7.0 %copy-start.3 = (bf16[1,3072]{1,0:T(2,128)(2,1)S(1)}, bf16[1,3072]{1,0:T(2,128)(2,1)}, u32[]{:S(2)}) copy-start(bf16[1,3072]{1,0:T(2,128)(2,1)} %get-tuple-element.72) | copy-start | bytes 18436 | tf_op jit(solution)/shard_map/cond
  85.7 26.2 %all-to-all-start.2 = ((bf16[16,12,3200]{2,1,0:T(8,128)(2,1)}), bf16[16,12,3200]{2,1,0:T(8,128)(2,1)S(1)}, u32[]{:S(2)}, u32[]{:S(2)}) async-start(bf16[16,12,3200]{2,1,0:T(8,128)(2,1)} %broadcast_in_dim.35), calls=%async_computation.2 | async-start | bytes 3276800 | tf_op jit(solution)/shard_map/cond/branch_1_fun/all_to_all | solution.py:8
  112.6 4.4 %copy-start.5 = (bf16[3072,384]{1,0:T(8,128)(2,1)S(1)}, bf16[3072,384]{1,0:T(8,128)(2,1)}, u32[]{:S(2)}) copy-start(bf16[3072,384]{1,0:T(8,128)(2,1)} %get-tuple-element.75) | copy-start | bytes 7077892 | tf_op jit(solution)/shard_map/cond
  117.0 0.9 copy-start.7
  131.9 7.1 %copy-start.1 = (s32[1,2,6,8]{3,1,2,0:T(2,128)S(1)}, s32[1,2,6,8]{3,1,2,0:T(2,128)}, u32[]{:S(2)}) copy-start(s32[1,2,6,8]{3,1,2,0:T(2,128)} %get-tuple-element.160) | copy-start | bytes 1156 | tf_op jit(solution)/shard_map/cond
  133.3 25.8 %all-to-all-start.3 = ((bf16[16,12,3072]{2,1,0:T(8,128)(2,1)}), bf16[16,12,3072]{2,1,0:T(8,128)(2,1)S(1)}, u32[]{:S(2)}, u32[]{:S(2)}) async-start(bf16[16,12,3072]{2,1,0:T(8,128)(2,1)} %reshape.94), calls=%async_computation.3 | async-start | bytes 3145728 | tf_op jit(solution)/shard_map/cond/branch_1_fun/all_to_all | solution.py:8

commit v2 on v1

v2 whole, which is shorter than its diff:
```python
import math

import jax
import jax.numpy as jnp
from jax import lax
from jax.experimental import pallas as pl
from jax.experimental.pallas import tpu as pltpu
from jax.sharding import PartitionSpec as P

LANES = 128
SUBLANES = 8
MIB = 1 << 20
AHEAD = 8
WHOLE = pl.BlockSpec(memory_space=pltpu.VMEM)
SCALAR = pl.BlockSpec(memory_space=pltpu.SMEM)
OUTSIDE = pl.BlockSpec(memory_space=pl.ANY)


def exchange(blocks, axes):
    return lax.all_to_all(blocks, axes, split_axis=0, concat_axis=0, tiled=True)


def unfold(folded, parts):
    rows, width = folded.shape[0] // parts, folded.shape[1]
    return folded.reshape(parts, rows, width).swapaxes(0, 1).reshape(rows, parts * width)


def sigmoid(v):
    return 1.0 / (1.0 + jnp.exp(-v))


def across(a, b):
    return lax.dot_general(a, b, (((1,), (1,)), ((), ())), preferred_element_type=jnp.float32)


def column_cuts(total, size):
    return [(at, min(size, total - at)) for at in range(0, total, size)]


def pack_kernel(parts, x_ref, ids_ref, sent_ref, kept_ref, block_ref):
    n_micro, per_group, top_count = ids_ref.shape
    rows = n_micro * per_group
    span = block_ref.shape[1] - LANES
    block_ref[:, span:] = jnp.full((parts * rows, LANES), -1.0, jnp.float32)
    for m in range(n_micro):
        block_ref[m * per_group : (m + 1) * per_group, span : span + top_count] = ids_ref[m].astype(jnp.float32)
    if len(x_ref.shape) == 3:
        for m in range(n_micro):
            mine = x_ref[m].astype(jnp.float32)
            for p in range(parts):
                at = p * rows + m * per_group
                block_ref[at : at + per_group, :span] = mine[:, p * span : (p + 1) * span]
    else:
        block_ref[:, :span] = x_ref[...].astype(jnp.float32)
    block = block_ref[...].astype(jnp.bfloat16)
    kept_ref[...] = block
    for g in range(sent_ref.shape[0]):
        sent_ref[g] = block


def base_kernel(n_real, top_count, parts, kept_ref, gain_ref, router_ref, base_ref):
    rows, span = base_ref.shape[0] // parts, base_ref.shape[1]
    block = kept_ref[...].astype(jnp.float32)
    pieces = [block[p * rows : (p + 1) * rows, :span] for p in range(parts)]
    ids = block[:rows, span:]
    spread = sum(jnp.sum(v * v, axis=-1, keepdims=True) for v in pieces) / (parts * span)
    scale = lax.rsqrt(spread + 1e-06)
    gains = [gain_ref[:, p * span : (p + 1) * span].astype(jnp.float32) for p in range(parts)]
    normed = [(v * scale * gain).astype(jnp.bfloat16) for v, gain in zip(pieces, gains)]
    logits = sum(across(v, router_ref[:, p * span : (p + 1) * span]) for p, v in enumerate(normed))
    gates = sigmoid(logits)
    id_range = lax.broadcasted_iota(jnp.int32, gates.shape, 1)
    named = id_range.astype(jnp.float32)
    picked = sum((ids[:, k : k + 1] == named).astype(jnp.float32) for k in range(top_count))
    share = jnp.sum(jnp.where(id_range >= n_real, picked * gates, 0.0), axis=-1, keepdims=True)
    for p in range(parts):
        base_ref[p * rows : (p + 1) * rows, :] = pieces[p] + share * normed[p].astype(jnp.float32)


def layer_kernel(rows, parts, place_ref, all_ref, gain_ref, router_ref, *refs):
    sources, out_ref = refs[:6], refs[6]
    d_gate, d_up, d_down, e_gate, e_up, e_down = refs[7:13]
    normed_ref, coef_ref, d_hidden, e_hidden, value_ref, sems = refs[13:]
    n_groups, _, padded = all_ref.shape
    span = out_ref.shape[2]
    width = parts * span
    place = place_ref[0]
    unit = 16 // math.gcd(rows, 16)
    unit = unit if n_groups % unit == 0 else n_groups

    plan = []
    for at, size in column_cuts(d_gate.shape[1], 512):
        plan += [(0, d_gate, at, size), (1, d_up, at, size)]
    for at, size in column_cuts(e_gate.shape[1], 256):
        plan += [(3, e_gate, at, size), (4, e_up, at, size)]
    for at, size in column_cuts(width, 768):
        plan += [(2, d_down, at, size), (5, e_down, at, size)]
    copies = {}
    for i, (which, held, at, size) in enumerate(plan):
        source = sources[which].at[:, pl.ds(at, size)]
        copies[which, at] = (i, pltpu.make_async_copy(source, held.at[:, pl.ds(at, size)], sems.at[i]))
    order = list(copies.values())
    for i, copy in order[:AHEAD]:
        copy.start()

    def arrive(which, at):
        i, copy = copies[which, at]
        copy.wait()
        if i + AHEAD < len(order):
            order[i + AHEAD][1].start()

    def load(step, carry):
        start = pl.multiple_of(step * unit * rows, 16)
        blocks = [all_ref[step * unit + u].astype(jnp.float32) for u in range(unit)]
        pieces = [
            jnp.concatenate([b[p * rows : (p + 1) * rows, :span] for b in blocks], axis=0) for p in range(parts)
        ]
        ids = jnp.concatenate([b[:rows, span:] for b in blocks], axis=0)
        named = jnp.sum((ids == place.astype(jnp.float32)).astype(jnp.float32), axis=-1, keepdims=True)
        spread = sum(jnp.sum(v * v, axis=-1, keepdims=True) for v in pieces) / width
        scale = lax.rsqrt(spread + 1e-06)
        for p, v in enumerate(pieces):
            gain = gain_ref[:, p * span : (p + 1) * span].astype(jnp.float32)
            normed_ref[pl.ds(start, unit * rows), p * span : (p + 1) * span] = (v * scale * gain).astype(jnp.bfloat16)
        coef_ref[pl.ds(start, unit * rows), :] = jnp.broadcast_to(named, (unit * rows, LANES))
        return carry

    lax.fori_loop(0, n_groups // unit, load, 0)

    logits = across(normed_ref[...], router_ref[...])
    mine = lax.broadcasted_iota(jnp.int32, logits.shape, 1) == place
    gate = jnp.sum(jnp.where(mine, sigmoid(logits), 0.0), axis=-1, keepdims=True)
    coef_ref[...] = coef_ref[...] * gate

    def hidden(first, w_gate, w_up, target, size):
        for at, size in column_cuts(target.shape[1], size):
            cols = slice(at, at + size)
            arrive(first, at)
            gate_part = jnp.dot(normed_ref[...], w_gate[:, cols], preferred_element_type=jnp.float32)
            arrive(first + 1, at)
            up_part = jnp.dot(normed_ref[...], w_up[:, cols], preferred_element_type=jnp.float32)
            target[:, cols] = (gate_part * sigmoid(gate_part) * up_part).astype(jnp.bfloat16)

    hidden(0, d_gate, d_up, d_hidden, 512)
    hidden(3, e_gate, e_up, e_hidden, 256)
    for at, size in column_cuts(width, 768):
        arrive(2, at)
        arrive(5, at)
        for sub, step in column_cuts(size, 256):
            cols = slice(at + sub, at + sub + step)
            dense = jnp.dot(d_hidden[...], d_down[:, cols], preferred_element_type=jnp.float32)
            routed = jnp.dot(e_hidden[...], e_down[:, cols], preferred_element_type=jnp.float32)
            value_ref[:, cols] = dense + coef_ref[:, :1] * routed

    def pack(step, carry):
        start = pl.multiple_of(step * unit * rows, 16)
        tall = value_ref[pl.ds(start, unit * rows), :]
        for u in range(unit):
            mine = tall[u * rows : (u + 1) * rows]
            block = jnp.concatenate([mine[:, p * span : (p + 1) * span] for p in range(parts)], axis=0)
            out_ref[step * unit + u] = block.astype(out_ref.dtype)
        return carry

    lax.fori_loop(0, n_groups // unit, pack, 0)


def combine_kernel(parts, got_ref, base_ref, folded_ref, flat_ref, total_ref):
    n_micro, per_group, width = flat_ref.shape
    rows, span = n_micro * per_group, base_ref.shape[1]
    total = base_ref[...]
    for g in range(got_ref.shape[0]):
        total = total + got_ref[g].astype(jnp.float32)
    folded_ref[...] = total.astype(jnp.bfloat16)
    total_ref[...] = total
    for m in range(n_micro):
        for p in range(parts):
            at = p * rows + m * per_group
            flat_ref[m, :, p * span : (p + 1) * span] = total_ref[at : at + per_group, :].astype(jnp.bfloat16)


def layer(fed, ids, gain, router_t, weights, parts):
    n_micro, per_group, top_count = ids.shape
    n_groups = lax.axis_size("ep")
    n_pairs = lax.axis_size("tp")
    place = lax.axis_index("ep")
    width = gain.shape[1]
    rows, span = n_micro * per_group, width // parts
    tall, wide = parts * rows, span + LANES
    count = n_groups * rows

    sent, kept = pl.pallas_call(
        lambda *refs: pack_kernel(parts, *refs),
        out_shape=[
            jax.ShapeDtypeStruct((n_groups, tall, wide), jnp.bfloat16),
            jax.ShapeDtypeStruct((tall, wide), jnp.bfloat16),
        ],
        in_specs=[WHOLE, WHOLE],
        out_specs=[WHOLE, WHOLE],
        scratch_shapes=[pltpu.VMEM((tall, wide), jnp.float32)],
        compiler_params=pltpu.CompilerParams(vmem_limit_bytes=16 * MIB),
        name="pack",
    )(fed, ids)
    gathered = exchange(sent, "ep")

    base = pl.pallas_call(
        lambda *refs: base_kernel(n_groups, top_count, parts, *refs),
        out_shape=jax.ShapeDtypeStruct((tall, span), jnp.float32),
        in_specs=[WHOLE] * 3,
        out_specs=WHOLE,
        compiler_params=pltpu.CompilerParams(vmem_limit_bytes=8 * MIB),
        cost_estimate=pl.CostEstimate(flops=int(1e8), bytes_accessed=int(1e6), transcendentals=0),
        name="base",
    )(kept, gain, router_t)

    n_dense, n_expert = weights[0].shape[1], weights[3].shape[1]
    partial = pl.pallas_call(
        lambda *refs: layer_kernel(rows, parts, *refs),
        out_shape=jax.ShapeDtypeStruct((n_groups, tall, span), jnp.bfloat16),
        in_specs=[SCALAR] + [WHOLE] * 3 + [OUTSIDE] * 6,
        out_specs=WHOLE,
        scratch_shapes=[pltpu.VMEM(w.shape, w.dtype) for w in weights]
        + [
            pltpu.VMEM((count, width), jnp.bfloat16),
            pltpu.VMEM((count, LANES), jnp.float32),
            pltpu.VMEM((count, n_dense), jnp.bfloat16),
            pltpu.VMEM((count, n_expert), jnp.bfloat16),
            pltpu.VMEM((count, width), jnp.float32),
            pltpu.SemaphoreType.DMA((64,)),
        ],
        compiler_params=pltpu.CompilerParams(vmem_limit_bytes=54 * MIB),
        cost_estimate=pl.CostEstimate(
            flops=6 * count * width * (n_dense + n_expert),
            bytes_accessed=6 * width * (n_dense + n_expert),
            transcendentals=0,
        ),
        name="layer",
    )(place.reshape(1).astype(jnp.int32), gathered, gain, router_t, *weights)

    share = tall // n_pairs
    received = exchange(partial.reshape(n_groups * n_pairs, share, span), ("ep", "tp"))
    if n_pairs > 1:
        kept_base = lax.dynamic_slice_in_dim(base, lax.axis_index("tp") * share, share, 0)
        part = (kept_base + jnp.sum(received.astype(jnp.float32), axis=0)).astype(jnp.bfloat16)
        folded = lax.all_gather(part, "tp", axis=0, tiled=True)
        return folded, unfold(folded, parts).reshape(n_micro, per_group, width)
    return pl.pallas_call(
        lambda *refs: combine_kernel(parts, *refs),
        out_shape=[
            jax.ShapeDtypeStruct((tall, span), jnp.bfloat16),
            jax.ShapeDtypeStruct((n_micro, per_group, width), jnp.bfloat16),
        ],
        in_specs=[WHOLE, WHOLE],
        out_specs=[WHOLE, WHOLE],
        scratch_shapes=[pltpu.VMEM((tall, span), jnp.float32)],
        compiler_params=pltpu.CompilerParams(vmem_limit_bytes=8 * MIB),
        name="combine",
    )(received, base)


def on_device(
    acts,
    route_ids,
    norm_gain,
    router,
    dense_gate,
    dense_up,
    dense_down,
    expert_gate,
    expert_up,
    expert_down,
):
    n_micro, per_group, width = acts.shape
    n_sections = lax.axis_size("pp")
    section = lax.axis_index("pp")
    rows = n_micro * per_group
    parts = SUBLANES // math.gcd(rows, SUBLANES)
    weights = (
        dense_gate[0],
        dense_up[0],
        dense_down[0],
        expert_gate[0, 0],
        expert_up[0, 0],
        expert_down[0, 0],
    )
    router_t = router[0].T

    fed = acts
    folded, flat = jnp.zeros((parts * rows, width // parts), jnp.bfloat16), acts
    for phase in range(n_sections):
        folded, flat = lax.cond(
            section == phase,
            lambda held, given: layer(given, route_ids[0], norm_gain, router_t, weights, parts),
            lambda held, given: held,
            (folded, flat),
            fed,
        )
        if phase + 1 < n_sections:
            fed = lax.ppermute(folded, "pp", [(phase, phase + 1)])
    return flat[None]


def solution(mesh):
    return jax.shard_map(
        on_device,
        mesh=mesh,
        in_specs=(
            P(None, "ep", None),
            P("pp", None, "ep", None),
            P("pp", None),
            P("pp", None, None),
            P("pp", None, ("ep", "tp")),
            P("pp", None, ("ep", "tp")),
            P("pp", ("ep", "tp"), None),
            P("pp", "ep", None, "tp"),
            P("pp", "ep", None, "tp"),
            P("pp", "ep", "tp", None),
        ),
        out_specs=P("pp", None, "ep", None),
        check_vma=False,
    )
```

time: 161 us -> 133 us (0.83)
  waiting for transfers between devices: 121 us -> 100 us
  matrix products: 19.6 us -> 0 us
  Pallas kernels: 0 us -> 18 us
  local copies, waits for them, and re-layouts: 5.65 us -> 2.32 us
    dot_general x6 -> x0, matrix products: 19.6 us -> none  [the longest x2 13.5 us: gated_block(): return jnp.dot(hidden, w_down, preferred_element_type=jnp.float32)]
    pallas_call x0 -> x4, Pallas kernels: none -> 18 us  [the longest x1 15.5 us: layer(): pl.pallas_call(lambda *refs: layer_kernel(rows, parts, *refs), out_shape=...]
    ppermute x1, waiting for transfers between devices: 81.2 us -> 67.6 us  [on_device(): fed = lax.ppermute(folded, 'pp', [(phase, phase + 1)])]
    all_to_all x2, waiting for transfers between devices: 39.7 us -> 32.4 us  [exchange(): return lax.all_to_all(blocks, axes, split_axis=0, concat_axis=0, tiled=True)]
    reshape x4 -> x0, local copies, waits for them, and re-layouts: 1.67 us -> none  [the longest x1 1.31 us: layer(): partial.astype(jnp.bfloat16).reshape(n_groups * n_pairs, share, width)]
where the time goes in v2:
time: 133 us; the launch traced here: 132 us
  waiting for transfers between devices  100 us (75%)
  Pallas kernels  18 us (14%)
  starting transfers between devices  11.8 us (9%)
  local copies, waits for them, and re-layouts  2.32 us (2%)
    ppermute x1, waiting for transfers between devices, on_device(): fed = lax.ppermute(folded, 'pp', [(phase, phase + 1)])  67.6 us
    all_to_all x2, waiting for transfers between devices, exchange(): return lax.all_to_all(blocks, axes, split_axis=0, concat_axis=0, tiled=True)  32.4 us
    pallas_call x1, Pallas kernels, layer(): pl.pallas_call(lambda *refs: layer_kernel(rows, parts, *refs), out_shape=...  15.5 us
    all_to_all x2, starting transfers between devices, exchange(): return lax.all_to_all(blocks, axes, split_axis=0, concat_axis=0, tiled=True)  10.5 us
  transfers between devices with their start and end apart: 3, of which 3 were waited for; matrix products, arithmetic and copies ran while one was open for 0% of the time, Pallas kernels for 0%

profile of v2, /device:TPU:1, one launch (start us, length us, event | category | flops | bytes accessed | tf_op | source)
XLA Modules:
  0.0 132.2 jit_solution(7722723999073565366)
XLA Ops:
  0.0 0.9 conditional.2
  0.0 0.9 copy.18
  0.9 1.3 collective-permute-start
  2.2 67.6 %collective-permute-done = bf16[24,1536]{1,0:T(8,128)(2,1)S(1)} collective-permute-done((bf16[24,1536]{1,0:T(8,128)(2,1)S(1)}, bf16[24,1536]{1,0:T(8,128)(2,1)S(1)}, u32[]{:S(2)}, u32[]{:S(2)}) %collective-permute-start) | collective-permute-done | bytes 73760 | tf_op jit(solution)/shard_map/ppermute | solution.py:298
  69.9 61.7 %conditional.3 = (bf16[2,6,3072]{2,1,0:T(8,128)(2,1)S(1)}) conditional(s32[]{:T(128)} %convert_element_type.6, bf16[2,6,3072]{2,1,0:T(8,128)(2,1)S(1)} %get-tuple-element.79, (s32[1,2,6,8]{3,1,2,0:T(2,128)}, bf16[24,1536]{1,0:T(8,128)(2,1)S(1)}, bf16[1,3072]{1,0:T(2,128)(2,1)}, bf16[24,3072]{1,0:T(8,128)(2,1)}, bf16[3072,384]{1,0:T(8,128)(2,1)}, ...), branch_computations={%region_2.0_spmd, %region_3.0_spmd} | conditional | flops 5082832896 | bytes 44377584 | solution.py:290
  69.9 0.7 copy.14.refs_1_
  70.6 1.2 pack.3
  71.7 0.0 copy-start.1
  71.7 0.0 copy-start.3
  71.7 0.0 copy-start.5
  71.7 5.3 %all-to-all-start.2 = ((bf16[16,24,1664]{2,1,0:T(8,128)(2,1)}), bf16[16,24,1664]{2,1,0:T(8,128)(2,1)}, u32[]{:S(2)}, u32[]{:S(2)}) async-start(bf16[16,24,1664]{2,1,0:T(8,128)(2,1)} %get-tuple-element.66), calls=%async_computation.2 | async-start | bytes 2555904 | tf_op jit(solution)/shard_map/cond/branch_1_fun/all_to_all | solution.py:20
  77.0 17.0 %all-to-all-done.2.refs_1_ = bf16[16,24,1664]{2,1,0:T(8,128)(2,1)} async-done(((bf16[16,24,1664]{2,1,0:T(8,128)(2,1)}), bf16[16,24,1664]{2,1,0:T(8,128)(2,1)}, u32[]{:S(2)}, u32[]{:S(2)}) %all-to-all-start.2) | async-done | bytes 1277984 | tf_op jit(solution)/shard_map/cond/branch_1_fun/all_to_all | solution.py:20
  94.0 0.0 copy-done.1
  94.0 0.0 copy-done.3
  94.0 0.0 copy-done.5
  94.0 15.5 %layer.3 = bf16[16,24,1536]{2,1,0:T(8,128)(2,1)} custom-call(s32[1]{0:T(128)} %bitcast.2.refs_0_, bf16[16,24,1664]{2,1,0:T(8,128)(2,1)} %all-to-all-done.2.refs_1_, bf16[1,3072]{1,0:T(2,128)(2,1)S(1)} %copy-done.5, bf16[24,3072]{1,0:T(8,128)(2,1)S(1)} %copy-done.3, bf16[3072,384]{1,0:T(8,128)(2,1)S(1)} %copy-done.1, ...), custom_call_target="tpu_custom_call" | custom-call | flops 4982833152 | bytes 25952256 | tf_op jit(solution)/shard_map/cond/branch_1_fun/layer/pallas_call | solution.py:216
  109.5 5.2 %all-to-all-start.3 = ((bf16[16,24,1536]{2,1,0:T(8,128)(2,1)}), bf16[16,24,1536]{2,1,0:T(8,128)(2,1)S(1)}, u32[]{:S(2)}, u32[]{:S(2)}) async-start(bf16[16,24,1536]{2,1,0:T(8,128)(2,1)} %layer.3), calls=%async_computation.3 | async-start | bytes 2359296 | tf_op jit(solution)/shard_map/cond/branch_1_fun/all_to_all | solution.py:20
  114.8 0.5 base.3.refs_1_
  115.3 15.4 %all-to-all-done.3.refs_0_ = bf16[16,24,1536]{2,1,0:T(8,128)(2,1)S(1)} async-done(((bf16[16,24,1536]{2,1,0:T(8,128)(2,1)}), bf16[16,24,1536]{2,1,0:T(8,128)(2,1)S(1)}, u32[]{:S(2)}, u32[]{:S(2)}) %all-to-all-start.3) | async-done | bytes 1179680 | tf_op jit(solution)/shard_map/cond/branch_1_fun/all_to_all | solution.py:20
  130.7 0.8 combine.3
  131.5 0.7 copy.17
  (1 shorter events, 0.0 us)
Async XLA Ops:
  0.9 68.9 %collective-permute-start = (bf16[24,1536]{1,0:T(8,128)(2,1)S(1)}, bf16[24,1536]{1,0:T(8,128)(2,1)S(1)}, u32[]{:S(2)}, u32[]{:S(2)}) collective-permute-start(bf16[24,1536]{1,0:T(8,128)(2,1)S(1)} %get-tuple-element.80), channel_id=1, source_target_pairs={{0,16},{1,17},{2,18},{3,19},{4,20},{5,21},{6,22},{7,23},{8,24},{9,... | collective-permute-start | bytes 221192 | tf_op jit(solution)/shard_map/ppermute | solution.py:298
  71.7 22.3 %copy-start.1 = (bf16[3072,384]{1,0:T(8,128)(2,1)S(1)}, bf16[3072,384]{1,0:T(8,128)(2,1)}, u32[]{:S(2)}) copy-start(bf16[3072,384]{1,0:T(8,128)(2,1)} %get-tuple-element.69.refs_4_) | copy-start | bytes 7077892 | tf_op jit(solution)/shard_map/cond
  71.7 22.3 %copy-start.3 = (bf16[24,3072]{1,0:T(8,128)(2,1)S(1)}, bf16[24,3072]{1,0:T(8,128)(2,1)}, u32[]{:S(2)}) copy-start(bf16[24,3072]{1,0:T(8,128)(2,1)} %get-tuple-element.68.refs_3_.refs_2_) | copy-start | bytes 442372 | tf_op jit(solution)/shard_map/cond
  71.7 22.3 %copy-start.5 = (bf16[1,3072]{1,0:T(2,128)(2,1)S(1)}, bf16[1,3072]{1,0:T(2,128)(2,1)}, u32[]{:S(2)}) copy-start(bf16[1,3072]{1,0:T(2,128)(2,1)} %get-tuple-element.67.refs_2_.refs_1_) | copy-start | bytes 18436 | tf_op jit(solution)/shard_map/cond
  71.7 22.3 %all-to-all-start.2 = ((bf16[16,24,1664]{2,1,0:T(8,128)(2,1)}), bf16[16,24,1664]{2,1,0:T(8,128)(2,1)}, u32[]{:S(2)}, u32[]{:S(2)}) async-start(bf16[16,24,1664]{2,1,0:T(8,128)(2,1)} %get-tuple-element.66), calls=%async_computation.2 | async-start | bytes 2555904 | tf_op jit(solution)/shard_map/cond/branch_1_fun/all_to_all | solution.py:20
  109.5 21.1 %all-to-all-start.3 = ((bf16[16,24,1536]{2,1,0:T(8,128)(2,1)}), bf16[16,24,1536]{2,1,0:T(8,128)(2,1)S(1)}, u32[]{:S(2)}, u32[]{:S(2)}) async-start(bf16[16,24,1536]{2,1,0:T(8,128)(2,1)} %layer.3), calls=%async_computation.3 | async-start | bytes 2359296 | tf_op jit(solution)/shard_map/cond/branch_1_fun/all_to_all | solution.py:20

commit v3 on v2

v3 whole, which is shorter than its diff:
```python
import math

import jax
import jax.numpy as jnp
from jax import lax
from jax.experimental import pallas as pl
from jax.experimental.pallas import tpu as pltpu
from jax.sharding import PartitionSpec as P

LANES = 128
SUBLANES = 8
MIB = 1 << 20
FLIGHT = 12 * MIB
PIECE = 3 * MIB // 4
HIDDEN = 256
OUT = 512
WHOLE = pl.BlockSpec(memory_space=pltpu.VMEM)
SCALAR = pl.BlockSpec(memory_space=pltpu.SMEM)
OUTSIDE = pl.BlockSpec(memory_space=pl.ANY)


def exchange(blocks, axes):
    return lax.all_to_all(blocks, axes, split_axis=0, concat_axis=0, tiled=True)


def unfold(folded, parts):
    tall = folded.shape[0]
    lines = []
    for at, _, height in regions(tall // parts, parts):
        pieces = [folded[at + p * height : at + (p + 1) * height] for p in range(parts)]
        lines.append(jnp.concatenate(pieces, axis=1))
    return jnp.concatenate(lines, axis=0)


def sigmoid(v):
    return 1.0 / (1.0 + jnp.exp(-v))


def across(a, b):
    return lax.dot_general(a, b, (((1,), (1,)), ((), ())), preferred_element_type=jnp.float32)


def spread_of(pieces):
    count = sum(v.shape[1] for v in pieces)
    return sum(jnp.sum(v * v, axis=-1, keepdims=True) for v in pieces) / count


def regions(rows, parts):
    even = rows // SUBLANES * SUBLANES
    found = [(0, 0, even), (parts * even, even, rows - even)]
    return [region for region in found if region[2] > 0]


def place_in_block(rows, parts, part, row):
    for at, first, height in regions(rows, parts):
        if first <= row < first + height:
            return at + part * height + row - first


def pair_shapes(width, count):
    if count % LANES == 0:
        return [(width, 2 * count), (SUBLANES, LANES)]
    return [(width, count)] * 2


def refs_joined(held, source):
    return held.shape[1] == 2 * source.shape[1]


def column_cuts(total, size):
    return [(at, min(size, total - at)) for at in range(0, total, size)]


def pack_kernel(parts, x_ref, ids_ref, sent_ref, kept_ref, block_ref):
    per_group, n_micro, top_count = ids_ref.shape
    rows = n_micro * per_group
    span = block_ref.shape[1] - LANES
    step = math.gcd(n_micro, SUBLANES)
    block_ref[:, span:] = jnp.full((parts * rows, LANES), -1.0, jnp.float32)
    for i in range(per_group):
        ids = ids_ref[i].astype(jnp.float32)
        for m in range(0, n_micro, step):
            at = place_in_block(rows, parts, 0, i * n_micro + m)
            block_ref[at : at + step, span : span + top_count] = ids[m : m + step]
    if len(x_ref.shape) == 3:
        for i in range(per_group):
            mine = x_ref[i].astype(jnp.float32)
            for m in range(0, n_micro, step):
                for p in range(parts):
                    at = place_in_block(rows, parts, p, i * n_micro + m)
                    block_ref[at : at + step, :span] = mine[m : m + step, p * span : (p + 1) * span]
    else:
        block_ref[:, :span] = x_ref[...].astype(jnp.float32)
    block = block_ref[...].astype(jnp.bfloat16)
    kept_ref[...] = block
    for g in range(sent_ref.shape[0]):
        sent_ref[g] = block


def base_kernel(n_real, top_count, parts, kept_ref, gain_ref, router_ref, base_ref):
    span = base_ref.shape[1]
    gains = [gain_ref[:, p * span : (p + 1) * span].astype(jnp.float32) for p in range(parts)]
    block = kept_ref[...].astype(jnp.float32)
    for at, _, height in regions(base_ref.shape[0] // parts, parts):
        pieces = [block[at + p * height : at + (p + 1) * height, :span] for p in range(parts)]
        ids = block[at : at + height, span:]
        scale = lax.rsqrt(spread_of(pieces) + 1e-06)
        normed = [(v * scale * gain).astype(jnp.bfloat16) for v, gain in zip(pieces, gains)]
        logits = sum(across(v, router_ref[:, p * span : (p + 1) * span]) for p, v in enumerate(normed))
        gates = sigmoid(logits)
        id_range = lax.broadcasted_iota(jnp.int32, gates.shape, 1)
        named = id_range.astype(jnp.float32)
        picked = sum((ids[:, k : k + 1] == named).astype(jnp.float32) for k in range(top_count))
        share = jnp.sum(jnp.where(id_range >= n_real, picked * gates, 0.0), axis=-1, keepdims=True)
        for p in range(parts):
            rows = slice(at + p * height, at + (p + 1) * height)
            base_ref[rows, :] = pieces[p] + share * normed[p].astype(jnp.float32)


def layer_kernel(rows, parts, place_ref, all_ref, gain_ref, router_ref, *refs):
    sources, out_ref = refs[:6], refs[6]
    held = refs[7:13]
    d_down, e_down = held[2], held[5]
    normed_ref, coef_ref, d_hidden, e_hidden, value_ref, stage_ref, sems, out_sems = refs[13:]
    n_groups = all_ref.shape[0]
    span = out_ref.shape[2]
    width = parts * span
    place = place_ref[0]
    unit = 16 // math.gcd(rows, 16)
    unit = unit if n_groups % unit == 0 else n_groups

    out_cuts = column_cuts(span, OUT)
    if span % OUT == 0 and OUT % (2 * LANES) == 0:
        out_cuts = out_cuts[:-1] + [(span - OUT, OUT // 2), (span - OUT // 2, OUT // 2)]
    plan = []
    for which, hidden_ref in ((0, d_hidden), (3, e_hidden)):
        joined = hidden_ref.shape[1] % LANES == 0
        for at, size in column_cuts(hidden_ref.shape[1], HIDDEN):
            spots = (2 * at, 2 * at + size) if joined else (at, at)
            plan += [(which, at, spots[0], size), (which + 1, at, spots[1], size)]
    for at, size in out_cuts:
        plan += [(which, p * span + at, p * span + at, size) for which in (2, 5) for p in range(parts)]
    held = tuple(
        held[i - 1] if i in (1, 4) and refs_joined(held[i - 1], sources[i]) else h for i, h in enumerate(held)
    )
    order, owned, volume, total = [], {}, [], 0
    for which, at, put, size in plan:
        height = held[which].shape[0]
        pieces = max(1, height * size * 2 // PIECE)
        pieces = pieces if height % pieces == 0 and height // pieces % 16 == 0 else 1
        owned[which, at] = range(len(order), len(order) + pieces)
        for k in range(pieces):
            lines = pl.ds(k * (height // pieces), height // pieces)
            source, target = sources[which].at[lines, pl.ds(at, size)], held[which].at[lines, pl.ds(put, size)]
            order.append(pltpu.make_async_copy(source, target, sems.at[len(order)]))
            total += height // pieces * size * 2
            volume.append(total)
    begun = [0]

    def start_until(limit):
        while begun[0] < len(order) and volume[begun[0]] <= limit:
            order[begun[0]].start()
            begun[0] += 1

    start_until(max(FLIGHT, volume[0]))

    def arrive(which, at):
        for i in owned[which, at]:
            order[i].wait()
            start_until(volume[i] + FLIGHT)

    def load(step, carry):
        blocks = [all_ref[step * unit + u].astype(jnp.float32) for u in range(unit)]
        for at, first, height in regions(rows, parts):
            start = pl.multiple_of(n_groups * first + step * unit * height, 16)
            here = pl.ds(start, unit * height)
            pieces = [
                jnp.concatenate([b[at + p * height : at + (p + 1) * height, :span] for b in blocks], axis=0)
                for p in range(parts)
            ]
            ids = jnp.concatenate([b[at : at + height, span:] for b in blocks], axis=0)
            named = jnp.sum((ids == place.astype(jnp.float32)).astype(jnp.float32), axis=-1, keepdims=True)
            scale = lax.rsqrt(spread_of(pieces) + 1e-06)
            for p, v in enumerate(pieces):
                gain = gain_ref[:, p * span : (p + 1) * span].astype(jnp.float32)
                normed_ref[here, p * span : (p + 1) * span] = (v * scale * gain).astype(jnp.bfloat16)
            coef_ref[here, :] = jnp.broadcast_to(named, (unit * height, LANES))
        return carry

    lax.fori_loop(0, n_groups // unit, load, 0)

    logits = across(normed_ref[...], router_ref[...])
    mine = lax.broadcasted_iota(jnp.int32, logits.shape, 1) == place
    gate = jnp.sum(jnp.where(mine, sigmoid(logits), 0.0), axis=-1, keepdims=True)
    coef_ref[...] = coef_ref[...] * gate

    def hidden(which, target):
        joined = target.shape[1] % LANES == 0
        for at, size in column_cuts(target.shape[1], HIDDEN):
            arrive(which, at)
            arrive(which + 1, at)
            if joined:
                pair = jnp.dot(
                    normed_ref[...], held[which][:, 2 * at : 2 * (at + size)], preferred_element_type=jnp.float32
                )
                gate_part, up_part = pair[:, :size], pair[:, size:]
            else:
                gate_part, up_part = (
                    jnp.dot(normed_ref[...], held[w][:, at : at + size], preferred_element_type=jnp.float32)
                    for w in (which, which + 1)
                )
            target[:, at : at + size] = (gate_part * sigmoid(gate_part) * up_part).astype(jnp.bfloat16)

    hidden(0, d_hidden)
    hidden(3, e_hidden)

    leaving = []
    for at, size in out_cuts:
        for which in (2, 5):
            for p in range(parts):
                arrive(which, p * span + at)
        for p in range(parts):
            cols = slice(p * span + at, p * span + at + size)
            dense = jnp.dot(d_hidden[...], d_down[:, cols], preferred_element_type=jnp.float32)
            routed = jnp.dot(e_hidden[...], e_down[:, cols], preferred_element_type=jnp.float32)
            value_ref[:, p * OUT : p * OUT + size] = dense + coef_ref[:, :1] * routed

        def pack(step, carry):
            rows_of = []
            for _, first, height in regions(rows, parts):
                start = pl.multiple_of(n_groups * first + step * unit * height, SUBLANES)
                rows_of.append((height, value_ref[pl.ds(start, unit * height), :]))
            for u in range(unit):
                pieces = [
                    tall[u * height : (u + 1) * height, p * OUT : p * OUT + size]
                    for height, tall in rows_of
                    for p in range(parts)
                ]
                block = jnp.concatenate(pieces, axis=0).astype(out_ref.dtype)
                stage_ref[step * unit + u, :, at : at + size] = block
            return carry

        lax.fori_loop(0, n_groups // unit, pack, 0)
        cols = pl.ds(at, size)
        leaving.append(pltpu.make_async_copy(stage_ref.at[:, :, cols], out_ref.at[:, :, cols], out_sems.at[len(leaving)]))
        leaving[-1].start()
    for copy in leaving:
        copy.wait()


def combine_kernel(parts, got_ref, base_ref, folded_ref, flat_ref, total_ref):
    per_group, n_micro, width = flat_ref.shape
    rows, span = n_micro * per_group, base_ref.shape[1]
    total = base_ref[...]
    for g in range(got_ref.shape[0]):
        total = total + got_ref[g].astype(jnp.float32)
    folded_ref[...] = total.astype(jnp.bfloat16)
    total_ref[...] = total
    step = math.gcd(n_micro, SUBLANES)
    for i in range(per_group):
        for m in range(0, n_micro, step):
            for p in range(parts):
                at = place_in_block(rows, parts, p, i * n_micro + m)
                cols = slice(p * span, (p + 1) * span)
                flat_ref[i, m : m + step, cols] = total_ref[at : at + step, :].astype(jnp.bfloat16)


def layer(fed, ids, gain, router_t, weights, parts):
    per_group, n_micro, top_count = ids.shape
    n_groups = lax.axis_size("ep")
    n_pairs = lax.axis_size("tp")
    place = lax.axis_index("ep")
    width = gain.shape[1]
    rows, span = n_micro * per_group, width // parts
    tall, wide = parts * rows, span + LANES
    count = n_groups * rows

    sent, kept = pl.pallas_call(
        lambda *refs: pack_kernel(parts, *refs),
        out_shape=[
            jax.ShapeDtypeStruct((n_groups, tall, wide), jnp.bfloat16),
            jax.ShapeDtypeStruct((tall, wide), jnp.bfloat16),
        ],
        in_specs=[WHOLE, WHOLE],
        out_specs=[WHOLE, WHOLE],
        scratch_shapes=[pltpu.VMEM((tall, wide), jnp.float32)],
        compiler_params=pltpu.CompilerParams(vmem_limit_bytes=16 * MIB),
        name="pack",
    )(fed, ids)
    gathered = exchange(sent, "ep")

    base = pl.pallas_call(
        lambda *refs: base_kernel(n_groups, top_count, parts, *refs),
        out_shape=jax.ShapeDtypeStruct((tall, span), jnp.float32),
        in_specs=[WHOLE] * 3,
        out_specs=WHOLE,
        compiler_params=pltpu.CompilerParams(vmem_limit_bytes=8 * MIB),
        cost_estimate=pl.CostEstimate(flops=int(1e8), bytes_accessed=int(1e6), transcendentals=0),
        name="base",
    )(kept, gain, router_t)

    n_dense, n_expert = weights[0].shape[1], weights[3].shape[1]
    partial = pl.pallas_call(
        lambda *refs: layer_kernel(rows, parts, *refs),
        out_shape=jax.ShapeDtypeStruct((n_groups, tall, span), jnp.bfloat16),
        in_specs=[SCALAR] + [WHOLE] * 3 + [OUTSIDE] * 6,
        out_specs=OUTSIDE,
        scratch_shapes=[
            *(pltpu.VMEM(shape, jnp.bfloat16) for shape in pair_shapes(width, n_dense)),
            pltpu.VMEM((n_dense, width), jnp.bfloat16),
            *(pltpu.VMEM(shape, jnp.bfloat16) for shape in pair_shapes(width, n_expert)),
            pltpu.VMEM((n_expert, width), jnp.bfloat16),
            pltpu.VMEM((count, width), jnp.bfloat16),
            pltpu.VMEM((count, LANES), jnp.float32),
            pltpu.VMEM((count, n_dense), jnp.bfloat16),
            pltpu.VMEM((count, n_expert), jnp.bfloat16),
            pltpu.VMEM((count, parts * OUT), jnp.float32),
            pltpu.VMEM((n_groups, tall, span), jnp.bfloat16),
            pltpu.SemaphoreType.DMA((128,)),
            pltpu.SemaphoreType.DMA((16,)),
        ],
        compiler_params=pltpu.CompilerParams(vmem_limit_bytes=50 * MIB),
        cost_estimate=pl.CostEstimate(
            flops=6 * count * width * (n_dense + n_expert),
            bytes_accessed=6 * width * (n_dense + n_expert),
            transcendentals=0,
        ),
        name="layer",
    )(place.reshape(1).astype(jnp.int32), gathered, gain, router_t, *weights)

    share = tall // n_pairs
    received = exchange(partial.reshape(n_groups * n_pairs, share, span), ("ep", "tp"))
    if n_pairs > 1:
        kept_base = lax.dynamic_slice_in_dim(base, lax.axis_index("tp") * share, share, 0)
        part = (kept_base + jnp.sum(received.astype(jnp.float32), axis=0)).astype(jnp.bfloat16)
        folded = lax.all_gather(part, "tp", axis=0, tiled=True)
        return folded, unfold(folded, parts).reshape(per_group, n_micro, width)
    return pl.pallas_call(
        lambda *refs: combine_kernel(parts, *refs),
        out_shape=[
            jax.ShapeDtypeStruct((tall, span), jnp.bfloat16),
            jax.ShapeDtypeStruct((per_group, n_micro, width), jnp.bfloat16),
        ],
        in_specs=[WHOLE, WHOLE],
        out_specs=[WHOLE, WHOLE],
        scratch_shapes=[pltpu.VMEM((tall, span), jnp.float32)],
        compiler_params=pltpu.CompilerParams(vmem_limit_bytes=8 * MIB),
        name="combine",
    )(received, base)


def on_device(
    acts,
    route_ids,
    norm_gain,
    router,
    dense_gate,
    dense_up,
    dense_down,
    expert_gate,
    expert_up,
    expert_down,
):
    n_micro, per_group, width = acts.shape
    n_sections = lax.axis_size("pp")
    section = lax.axis_index("pp")
    rows = n_micro * per_group
    parts = SUBLANES // math.gcd(rows, SUBLANES)
    weights = (
        dense_gate[0],
        dense_up[0],
        dense_down[0],
        expert_gate[0, 0],
        expert_up[0, 0],
        expert_down[0, 0],
    )
    router_t = router[0].T

    fed = acts.swapaxes(0, 1)
    ids = route_ids[0].swapaxes(0, 1)
    kept = None
    for phase in range(n_sections):
        folded, flat = lax.cond(
            section == phase,
            lambda held, given: layer(given, ids, norm_gain, router_t, weights, parts),
            lambda held, given: held or (
                jnp.zeros((parts * rows, width // parts), jnp.bfloat16),
                jnp.zeros((per_group, n_micro, width), jnp.bfloat16),
            ),
            kept,
            fed,
        )
        kept = (folded, flat)
        if phase + 1 < n_sections:
            fed = lax.ppermute(folded, "pp", [(phase, phase + 1)])
    return flat.swapaxes(0, 1)[None]


def solution(mesh):
    return jax.shard_map(
        on_device,
        mesh=mesh,
        in_specs=(
            P(None, "ep", None),
            P("pp", None, "ep", None),
            P("pp", None),
            P("pp", None, None),
            P("pp", None, ("ep", "tp")),
            P("pp", None, ("ep", "tp")),
            P("pp", ("ep", "tp"), None),
            P("pp", "ep", None, "tp"),
            P("pp", "ep", None, "tp"),
            P("pp", "ep", "tp", None),
        ),
        out_specs=P("pp", None, "ep", None),
        check_vma=False,
    )
```

time: 133 us -> 125 us (0.940)
  waiting for transfers between devices: 100 us -> 96.5 us
  Pallas kernels: 18 us -> 15.3 us
  local copies, waits for them, and re-layouts: 2.32 us -> 0.69 us
    pallas_call x1, Pallas kernels: 15.5 us -> 12 us  [layer(): pl.pallas_call(lambda *refs: layer_kernel(rows, parts, *refs), out_shape=...]
    ppermute x1, waiting for transfers between devices: 67.6 us -> 64.2 us  [on_device(): fed = lax.ppermute(folded, 'pp', [(phase, phase + 1)])]
    unnamed x2 -> x0, local copies, waits for them, and re-layouts: 1.61 us -> none
where the time goes in v3:
time: 125 us; the launch traced here: 124 us
  waiting for transfers between devices  96.5 us (77%)
  Pallas kernels  15.3 us (12%)
  starting transfers between devices  11.7 us (9%)
    ppermute x1, waiting for transfers between devices, on_device(): fed = lax.ppermute(folded, 'pp', [(phase, phase + 1)])  64.2 us
    all_to_all x2, waiting for transfers between devices, exchange(): return lax.all_to_all(blocks, axes, split_axis=0, concat_axis=0, tiled=True)  32.3 us
    pallas_call x1, Pallas kernels, layer(): pl.pallas_call(lambda *refs: layer_kernel(rows, parts, *refs), out_shape=...  12 us
    all_to_all x2, starting transfers between devices, exchange(): return lax.all_to_all(blocks, axes, split_axis=0, concat_axis=0, tiled=True)  10.5 us
  transfers between devices with their start and end apart: 3, of which 3 were waited for; matrix products, arithmetic and copies ran while one was open for 0% of the time, Pallas kernels for 0%

profile of v3, /device:TPU:1, one launch (start us, length us, event | category | flops | bytes accessed | tf_op | source)
XLA Modules:
  0.0 124.3 jit_solution(2644755300314413565)
XLA Ops:
  0.0 0.7 conditional.2
  0.0 0.7 broadcast.5
  0.7 1.3 %collective-permute-start = (bf16[24,1536]{1,0:T(8,128)(2,1)S(1)}, bf16[24,1536]{1,0:T(8,128)(2,1)S(1)}, u32[]{:S(2)}, u32[]{:S(2)}) collective-permute-start(bf16[24,1536]{1,0:T(8,128)(2,1)S(1)} %get-tuple-element.80), channel_id=1, source_target_pairs={{0,16},{1,17},{2,18},{3,19},{4,20},{5,21},{6,22},{7,23},{8,24},{9,... | collective-permute-start | bytes 221192 | tf_op jit(solution)/shard_map/ppermute | solution.py:395
  2.0 64.2 %collective-permute-done = bf16[24,1536]{1,0:T(8,128)(2,1)S(1)} collective-permute-done((bf16[24,1536]{1,0:T(8,128)(2,1)S(1)}, bf16[24,1536]{1,0:T(8,128)(2,1)S(1)}, u32[]{:S(2)}, u32[]{:S(2)}) %collective-permute-start) | collective-permute-done | bytes 73760 | tf_op jit(solution)/shard_map/ppermute | solution.py:395
  66.2 58.1 %conditional.3 = (bf16[6,2,3072]{2,1,0:T(2,128)(2,1)}) conditional(s32[]{:T(128)} %convert_element_type.6, bf16[6,2,3072]{2,1,0:T(2,128)(2,1)} %get-tuple-element.79, (bf16[24,1536]{1,0:T(8,128)(2,1)S(1)}, s32[6,2,8]{2,1,0:T(2,128)}, bf16[1,3072]{1,0:T(2,128)(2,1)}, bf16[24,3072]{1,0:T(8,128)(2,1)}, bf16[3072,384]{1,0:T(8,128)(2,1)}, ...), branch_computations={%region_2.0_spmd, %region_3.0_spmd} | conditional | flops 5082832896 | bytes 34939604 | solution.py:383
  66.2 1.9 %pack.3 = (bf16[16,24,1664]{2,1,0:T(8,128)(2,1)}, bf16[24,1664]{1,0:T(8,128)(2,1)S(1)}) custom-call(bf16[24,1536]{1,0:T(8,128)(2,1)S(1)} %get-tuple-element.64.refs_0_, s32[6,2,8]{2,1,0:T(2,128)} %get-tuple-element.65.refs_1_), custom_call_target="tpu_custom_call" | custom-call | tf_op jit(solution)/shard_map/cond/branch_1_fun/pack/pallas_call | solution.py:278
  68.1 0.0 copy-start.1
  68.1 0.0 copy-start.3
  68.1 5.2 %all-to-all-start.2 = ((bf16[16,24,1664]{2,1,0:T(8,128)(2,1)}), bf16[16,24,1664]{2,1,0:T(8,128)(2,1)S(1)}, u32[]{:S(2)}, u32[]{:S(2)}) async-start(bf16[16,24,1664]{2,1,0:T(8,128)(2,1)} %get-tuple-element.66), calls=%async_computation.2 | async-start | bytes 2555904 | tf_op jit(solution)/shard_map/cond/branch_1_fun/all_to_all | solution.py:23
  73.3 16.9 %all-to-all-done.2.refs_1_ = bf16[16,24,1664]{2,1,0:T(8,128)(2,1)S(1)} async-done(((bf16[16,24,1664]{2,1,0:T(8,128)(2,1)}), bf16[16,24,1664]{2,1,0:T(8,128)(2,1)S(1)}, u32[]{:S(2)}, u32[]{:S(2)}) %all-to-all-start.2) | async-done | bytes 1277984 | tf_op jit(solution)/shard_map/cond/branch_1_fun/all_to_all | solution.py:23
  90.2 0.0 copy-done.1
  90.2 0.0 copy-done.3
  90.2 12.0 %layer.3 = bf16[16,24,1536]{2,1,0:T(8,128)(2,1)} custom-call(s32[1]{0:T(128)} %bitcast.1.refs_0_, bf16[16,24,1664]{2,1,0:T(8,128)(2,1)S(1)} %all-to-all-done.2.refs_1_, bf16[1,3072]{1,0:T(2,128)(2,1)S(1)} %copy-done.3, bf16[24,3072]{1,0:T(8,128)(2,1)S(1)} %copy-done.1, bf16[3072,384]{1,0:T(8,128)(2,1)} %get-tuple-element.69.refs_4_, ...), custom_call_target="tpu_custom_call" | custom-call | flops 4982833152 | bytes 25952256 | tf_op jit(solution)/shard_map/cond/branch_1_fun/layer/pallas_call | solution.py:303
  102.3 5.2 %all-to-all-start.3 = ((bf16[16,24,1536]{2,1,0:T(8,128)(2,1)}), bf16[16,24,1536]{2,1,0:T(8,128)(2,1)S(1)}, u32[]{:S(2)}, u32[]{:S(2)}) async-start(bf16[16,24,1536]{2,1,0:T(8,128)(2,1)} %layer.3), calls=%async_computation.3 | async-start | bytes 2359296 | tf_op jit(solution)/shard_map/cond/branch_1_fun/all_to_all | solution.py:23
  107.5 0.5 base.3.refs_1_
  108.0 15.4 %all-to-all-done.3.refs_0_ = bf16[16,24,1536]{2,1,0:T(8,128)(2,1)S(1)} async-done(((bf16[16,24,1536]{2,1,0:T(8,128)(2,1)}), bf16[16,24,1536]{2,1,0:T(8,128)(2,1)S(1)}, u32[]{:S(2)}, u32[]{:S(2)}) %all-to-all-start.3) | async-done | bytes 1179680 | tf_op jit(solution)/shard_map/cond/branch_1_fun/all_to_all | solution.py:23
  123.4 0.9 combine.3
  (1 shorter events, 0.0 us)
Async XLA Ops:
  0.7 65.5 %collective-permute-start = (bf16[24,1536]{1,0:T(8,128)(2,1)S(1)}, bf16[24,1536]{1,0:T(8,128)(2,1)S(1)}, u32[]{:S(2)}, u32[]{:S(2)}) collective-permute-start(bf16[24,1536]{1,0:T(8,128)(2,1)S(1)} %get-tuple-element.80), channel_id=1, source_target_pairs={{0,16},{1,17},{2,18},{3,19},{4,20},{5,21},{6,22},{7,23},{8,24},{9,... | collective-permute-start | bytes 221192 | tf_op jit(solution)/shard_map/ppermute | solution.py:395
  68.1 22.2 %copy-start.1 = (bf16[24,3072]{1,0:T(8,128)(2,1)S(1)}, bf16[24,3072]{1,0:T(8,128)(2,1)}, u32[]{:S(2)}) copy-start(bf16[24,3072]{1,0:T(8,128)(2,1)} %get-tuple-element.68.refs_3_.refs_2_) | copy-start | bytes 442372 | tf_op jit(solution)/shard_map/cond
  68.1 22.2 %copy-start.3 = (bf16[1,3072]{1,0:T(2,128)(2,1)S(1)}, bf16[1,3072]{1,0:T(2,128)(2,1)}, u32[]{:S(2)}) copy-start(bf16[1,3072]{1,0:T(2,128)(2,1)} %get-tuple-element.67.refs_2_.refs_1_) | copy-start | bytes 18436 | tf_op jit(solution)/shard_map/cond
  68.1 22.2 %all-to-all-start.2 = ((bf16[16,24,1664]{2,1,0:T(8,128)(2,1)}), bf16[16,24,1664]{2,1,0:T(8,128)(2,1)S(1)}, u32[]{:S(2)}, u32[]{:S(2)}) async-start(bf16[16,24,1664]{2,1,0:T(8,128)(2,1)} %get-tuple-element.66), calls=%async_computation.2 | async-start | bytes 2555904 | tf_op jit(solution)/shard_map/cond/branch_1_fun/all_to_all | solution.py:23
  102.3 21.1 %all-to-all-start.3 = ((bf16[16,24,1536]{2,1,0:T(8,128)(2,1)}), bf16[16,24,1536]{2,1,0:T(8,128)(2,1)S(1)}, u32[]{:S(2)}, u32[]{:S(2)}) async-start(bf16[16,24,1536]{2,1,0:T(8,128)(2,1)} %layer.3), calls=%async_computation.3 | async-start | bytes 2359296 | tf_op jit(solution)/shard_map/cond/branch_1_fun/all_to_all | solution.py:23

commit v4 on v3

--- a/solution.py
+++ b/solution.py
@@ -14,6 +14,7 @@
 PIECE = 3 * MIB // 4
 HIDDEN = 256
 OUT = 512
+REFS = 21
 WHOLE = pl.BlockSpec(memory_space=pltpu.VMEM)
 SCALAR = pl.BlockSpec(memory_space=pltpu.SMEM)
 OUTSIDE = pl.BlockSpec(memory_space=pl.ANY)
@@ -71,39 +72,71 @@
     return [(at, min(size, total - at)) for at in range(0, total, size)]
 
 
-def pack_kernel(parts, x_ref, ids_ref, sent_ref, kept_ref, block_ref):
+def write_tags(ids_ref, rows, parts, tags_ref):
     per_group, n_micro, top_count = ids_ref.shape
-    rows = n_micro * per_group
-    span = block_ref.shape[1] - LANES
     step = math.gcd(n_micro, SUBLANES)
-    block_ref[:, span:] = jnp.full((parts * rows, LANES), -1.0, jnp.float32)
+    tags_ref[...] = jnp.full(tags_ref.shape, -1.0, jnp.float32)
     for i in range(per_group):
         ids = ids_ref[i].astype(jnp.float32)
         for m in range(0, n_micro, step):
             at = place_in_block(rows, parts, 0, i * n_micro + m)
-            block_ref[at : at + step, span : span + top_count] = ids[m : m + step]
-    if len(x_ref.shape) == 3:
-        for i in range(per_group):
-            mine = x_ref[i].astype(jnp.float32)
-            for m in range(0, n_micro, step):
-                for p in range(parts):
-                    at = place_in_block(rows, parts, p, i * n_micro + m)
-                    block_ref[at : at + step, :span] = mine[m : m + step, p * span : (p + 1) * span]
-    else:
-        block_ref[:, :span] = x_ref[...].astype(jnp.float32)
-    block = block_ref[...].astype(jnp.bfloat16)
+            tags_ref[at : at + step, :top_count] = ids[m : m + step]
+
+
+def tags_kernel(parts, ids_ref, sent_ref, kept_ref, tags_ref):
+    write_tags(ids_ref, tags_ref.shape[0] // parts, parts, tags_ref)
+    block = tags_ref[...].astype(jnp.bfloat16)
     kept_ref[...] = block
     for g in range(sent_ref.shape[0]):
         sent_ref[g] = block
 
 
-def base_kernel(n_real, top_count, parts, kept_ref, gain_ref, router_ref, base_ref):
+def settle_kernel(tags_ref, out_ref, sem):
+    copy = pltpu.make_async_copy(tags_ref, out_ref, sem)
+    copy.start()
+    copy.wait()
+
+
+def first_pack_kernel(parts, x_hbm, ids_hbm, sent_ref, kept_ref, kept_tags_ref, x_ref, ids_ref, tags_ref, block_ref, sems):
+    copies = [
+        pltpu.make_async_copy(x_hbm, x_ref, sems.at[0]),
+        pltpu.make_async_copy(ids_hbm, ids_ref, sems.at[1]),
+    ]
+    for copy in copies:
+        copy.start()
+    for copy in copies:
+        copy.wait()
+    per_group, n_micro, _ = x_ref.shape
+    rows, span = per_group * n_micro, block_ref.shape[1]
+    step = math.gcd(n_micro, SUBLANES)
+    write_tags(ids_ref, rows, parts, tags_ref)
+    for i in range(per_group):
+        mine = x_ref[i].astype(jnp.float32)
+        for m in range(0, n_micro, step):
+            for p in range(parts):
+                at = place_in_block(rows, parts, p, i * n_micro + m)
+                block_ref[at : at + step, :] = mine[m : m + step, p * span : (p + 1) * span]
+    block, tags = block_ref[...].astype(jnp.bfloat16), tags_ref[...].astype(jnp.bfloat16)
+    kept_ref[...] = block
+    kept_tags_ref[...] = tags
+    for g in range(sent_ref.shape[0]):
+        sent_ref[g, :, :span] = block
+        sent_ref[g, :, span:] = tags
+
+
+def later_pack_kernel(x_ref, sent_ref):
+    for g in range(sent_ref.shape[0]):
+        sent_ref[g] = x_ref[...]
+
+
+def base_kernel(n_real, top_count, parts, kept_ref, tags_ref, gain_ref, router_ref, base_ref, blank_ref):
+    blank_ref[...] = jnp.zeros(blank_ref.shape, blank_ref.dtype)
     span = base_ref.shape[1]
     gains = [gain_ref[:, p * span : (p + 1) * span].astype(jnp.float32) for p in range(parts)]
-    block = kept_ref[...].astype(jnp.float32)
+    block, tags = kept_ref[...].astype(jnp.float32), tags_ref[...].astype(jnp.float32)
     for at, _, height in regions(base_ref.shape[0] // parts, parts):
-        pieces = [block[at + p * height : at + (p + 1) * height, :span] for p in range(parts)]
-        ids = block[at : at + height, span:]
+        pieces = [block[at + p * height : at + (p + 1) * height] for p in range(parts)]
+        ids = tags[at : at + height]
         scale = lax.rsqrt(spread_of(pieces) + 1e-06)
         normed = [(v * scale * gain).astype(jnp.bfloat16) for v, gain in zip(pieces, gains)]
         logits = sum(across(v, router_ref[:, p * span : (p + 1) * span]) for p, v in enumerate(normed))
@@ -118,6 +151,9 @@
 
 
 def layer_kernel(rows, parts, place_ref, all_ref, gain_ref, router_ref, *refs):
+    tags_ref = None
+    if len(refs) > REFS:
+        tags_ref, *refs = refs
     sources, out_ref = refs[:6], refs[6]
     held = refs[7:13]
     d_down, e_down = held[2], held[5]
@@ -171,6 +207,10 @@
 
     def load(step, carry):
         blocks = [all_ref[step * unit + u].astype(jnp.float32) for u in range(unit)]
+        if tags_ref is None:
+            tags = [b[:, span:] for b in blocks]
+        else:
+            tags = [tags_ref[step * unit + u].astype(jnp.float32) for u in range(unit)]
         for at, first, height in regions(rows, parts):
             start = pl.multiple_of(n_groups * first + step * unit * height, 16)
             here = pl.ds(start, unit * height)
@@ -178,7 +218,7 @@
                 jnp.concatenate([b[at + p * height : at + (p + 1) * height, :span] for b in blocks], axis=0)
                 for p in range(parts)
             ]
-            ids = jnp.concatenate([b[at : at + height, span:] for b in blocks], axis=0)
+            ids = jnp.concatenate([t[at : at + height] for t in tags], axis=0)
             named = jnp.sum((ids == place.astype(jnp.float32)).astype(jnp.float32), axis=-1, keepdims=True)
             scale = lax.rsqrt(spread_of(pieces) + 1e-06)
             for p, v in enumerate(pieces):
@@ -265,7 +305,7 @@
                 flat_ref[i, m : m + step, cols] = total_ref[at : at + step, :].astype(jnp.bfloat16)
 
 
-def layer(fed, ids, gain, router_t, weights, parts):
+def layer(fed, ids, known, gain, router_t, weights, parts):
     per_group, n_micro, top_count = ids.shape
     n_groups = lax.axis_size("ep")
     n_pairs = lax.axis_size("tp")
@@ -275,35 +315,60 @@
     tall, wide = parts * rows, span + LANES
     count = n_groups * rows
 
-    sent, kept = pl.pallas_call(
-        lambda *refs: pack_kernel(parts, *refs),
+    params = pltpu.CompilerParams(vmem_limit_bytes=16 * MIB)
+    if known is None:
+        sent, kept, tags = pl.pallas_call(
+            lambda *refs: first_pack_kernel(parts, *refs),
+            out_shape=[
+                jax.ShapeDtypeStruct((n_groups, tall, wide), jnp.bfloat16),
+                jax.ShapeDtypeStruct((tall, span), jnp.bfloat16),
+                jax.ShapeDtypeStruct((tall, LANES), jnp.bfloat16),
+            ],
+            in_specs=[OUTSIDE, OUTSIDE],
+            out_specs=[WHOLE] * 3,
+            scratch_shapes=[
+                pltpu.VMEM(fed.shape, fed.dtype),
+                pltpu.VMEM(ids.shape, ids.dtype),
+                pltpu.VMEM((tall, LANES), jnp.float32),
+                pltpu.VMEM((tall, span), jnp.float32),
+                pltpu.SemaphoreType.DMA((2,)),
+            ],
+            compiler_params=params,
+            name="pack",
+        )(fed, ids)
+        all_tags = []
+    else:
+        kept, tags, all_tags = fed, known[0], [known[1]]
+        sent = pl.pallas_call(
+            later_pack_kernel,
+            out_shape=jax.ShapeDtypeStruct((n_groups, tall, span), jnp.bfloat16),
+            in_specs=[WHOLE],
+            out_specs=WHOLE,
+            compiler_params=params,
+            name="pack",
+        )(fed)
+    gathered = exchange(sent, "ep")
+
+    blank_groups = n_groups if known is None else 1
+    base, blank = pl.pallas_call(
+        lambda *refs: base_kernel(n_groups, top_count, parts, *refs),
         out_shape=[
-            jax.ShapeDtypeStruct((n_groups, tall, wide), jnp.bfloat16),
-            jax.ShapeDtypeStruct((tall, wide), jnp.bfloat16),
+            jax.ShapeDtypeStruct((tall, span), jnp.float32),
+            jax.ShapeDtypeStruct((blank_groups, tall, LANES), jnp.bfloat16),
         ],
-        in_specs=[WHOLE, WHOLE],
+        in_specs=[WHOLE] * 4,
         out_specs=[WHOLE, WHOLE],
-        scratch_shapes=[pltpu.VMEM((tall, wide), jnp.float32)],
-        compiler_params=pltpu.CompilerParams(vmem_limit_bytes=16 * MIB),
-        name="pack",
-    )(fed, ids)
-    gathered = exchange(sent, "ep")
-
-    base = pl.pallas_call(
-        lambda *refs: base_kernel(n_groups, top_count, parts, *refs),
-        out_shape=jax.ShapeDtypeStruct((tall, span), jnp.float32),
-        in_specs=[WHOLE] * 3,
-        out_specs=WHOLE,
         compiler_params=pltpu.CompilerParams(vmem_limit_bytes=8 * MIB),
         cost_estimate=pl.CostEstimate(flops=int(1e8), bytes_accessed=int(1e6), transcendentals=0),
         name="base",
-    )(kept, gain, router_t)
+    )(kept, tags, gain, router_t)
 
     n_dense, n_expert = weights[0].shape[1], weights[3].shape[1]
+    weights = [pltpu.with_memory_space_constraint(w, pltpu.HBM) for w in weights]
     partial = pl.pallas_call(
         lambda *refs: layer_kernel(rows, parts, *refs),
         out_shape=jax.ShapeDtypeStruct((n_groups, tall, span), jnp.bfloat16),
-        in_specs=[SCALAR] + [WHOLE] * 3 + [OUTSIDE] * 6,
+        in_specs=[SCALAR] + [WHOLE] * (3 + len(all_tags)) + [pl.BlockSpec(memory_space=pltpu.HBM)] * 6,
         out_specs=OUTSIDE,
         scratch_shapes=[
             *(pltpu.VMEM(shape, jnp.bfloat16) for shape in pair_shapes(width, n_dense)),
@@ -326,7 +391,7 @@
             transcendentals=0,
         ),
         name="layer",
-    )(place.reshape(1).astype(jnp.int32), gathered, gain, router_t, *weights)
+    )(place.reshape(1).astype(jnp.int32), gathered, gain, router_t, *all_tags, *weights)
 
     share = tall // n_pairs
     received = exchange(partial.reshape(n_groups * n_pairs, share, span), ("ep", "tp"))
@@ -334,8 +399,8 @@
         kept_base = lax.dynamic_slice_in_dim(base, lax.axis_index("tp") * share, share, 0)
         part = (kept_base + jnp.sum(received.astype(jnp.float32), axis=0)).astype(jnp.bfloat16)
         folded = lax.all_gather(part, "tp", axis=0, tiled=True)
-        return folded, unfold(folded, parts).reshape(per_group, n_micro, width)
-    return pl.pallas_call(
+        return folded, unfold(folded, parts).reshape(per_group, n_micro, width), blank
+    folded, flat = pl.pallas_call(
         lambda *refs: combine_kernel(parts, *refs),
         out_shape=[
             jax.ShapeDtypeStruct((tall, span), jnp.bfloat16),
@@ -347,6 +412,34 @@
         compiler_params=pltpu.CompilerParams(vmem_limit_bytes=8 * MIB),
         name="combine",
     )(received, base)
+    return folded, flat, blank
+
+
+def early_tags(ids, parts):
+    per_group, n_micro, _ = ids.shape
+    n_groups, tall = lax.axis_size("ep"), parts * per_group * n_micro
+    sent, tags = pl.pallas_call(
+        lambda *refs: tags_kernel(parts, *refs),
+        out_shape=[
+            jax.ShapeDtypeStruct((n_groups, tall, LANES), jnp.bfloat16),
+            jax.ShapeDtypeStruct((tall, LANES), jnp.bfloat16),
+        ],
+        in_specs=[WHOLE],
+        out_specs=[WHOLE, WHOLE],
+        scratch_shapes=[pltpu.VMEM((tall, LANES), jnp.float32)],
+        compiler_params=pltpu.CompilerParams(vmem_limit_bytes=8 * MIB),
+        name="tags",
+    )(ids)
+    settled = pl.pallas_call(
+        settle_kernel,
+        out_shape=pltpu.HBM(sent.shape, sent.dtype),
+        in_specs=[WHOLE],
+        out_specs=pl.BlockSpec(memory_space=pltpu.HBM),
+        scratch_shapes=[pltpu.SemaphoreType.DMA],
+        compiler_params=pltpu.CompilerParams(vmem_limit_bytes=8 * MIB),
+        name="settle",
+    )(exchange(sent, "ep"))
+    return tags, settled
 
 
 def on_device(
@@ -378,21 +471,27 @@
 
     fed = acts.swapaxes(0, 1)
     ids = route_ids[0].swapaxes(0, 1)
-    kept = None
-    for phase in range(n_sections):
+    n_groups = lax.axis_size("ep")
+    tall = parts * rows
+
+    def first(given):
+        folded, flat, blank = layer(given, ids, None, norm_gain, router_t, weights, parts)
+        return folded, flat, jnp.zeros((tall, LANES), jnp.bfloat16), blank
+
+    def idle(given):
+        folded = jnp.zeros((tall, width // parts), jnp.bfloat16)
+        return folded, jnp.zeros((per_group, n_micro, width), jnp.bfloat16), *early_tags(ids, parts)
+
+    folded, flat, *known = lax.cond(section == 0, first, idle, fed)
+    for phase in range(1, n_sections):
+        fed = lax.ppermute(folded, "pp", [(phase - 1, phase)])
         folded, flat = lax.cond(
             section == phase,
-            lambda held, given: layer(given, ids, norm_gain, router_t, weights, parts),
-            lambda held, given: held or (
-                jnp.zeros((parts * rows, width // parts), jnp.bfloat16),
-                jnp.zeros((per_group, n_micro, width), jnp.bfloat16),
-            ),
-            kept,
+            lambda held, given: layer(given, ids, known, norm_gain, router_t, weights, parts)[:2],
+            lambda held, given: held,
+            (folded, flat),
             fed,
         )
-        kept = (folded, flat)
-        if phase + 1 < n_sections:
-            fed = lax.ppermute(folded, "pp", [(phase, phase + 1)])
     return flat.swapaxes(0, 1)[None]
 
 

time: 125 us -> 123 us (0.984)
  waiting for transfers between devices: 96.5 us -> 80.2 us
  blocking collectives: 0 us -> 13.7 us
    ppermute x1, waiting for transfers between devices: 64.2 us -> 49.2 us  [on_device(): fed = lax.ppermute(folded, 'pp', [(phase - 1, phase)])]
    all_to_all x0 -> x1, blocking collectives: none -> 13.7 us  [exchange(): return lax.all_to_all(blocks, axes, split_axis=0, concat_axis=0, tiled=True)]
    all_to_all x2, waiting for transfers between devices: 32.3 us -> 31 us  [exchange(): return lax.all_to_all(blocks, axes, split_axis=0, concat_axis=0, tiled=True)]
  transfers between devices with their start and end apart: 3 -> 3, of which waited for: 3 -> 3; matrix products, arithmetic and copies ran while one was open for 0% -> 0% of each run, Pallas kernels for 0% -> 1%
where the time goes in v4:
time: 123 us; the launch traced here: 122 us
  waiting for transfers between devices  80.2 us (65%)
  Pallas kernels  16.1 us (13%)
  blocking collectives  13.7 us (11%)
  starting transfers between devices  11.6 us (9%)
    ppermute x1, waiting for transfers between devices, on_device(): fed = lax.ppermute(folded, 'pp', [(phase - 1, phase)])  49.2 us
    all_to_all x2, waiting for transfers between devices, exchange(): return lax.all_to_all(blocks, axes, split_axis=0, concat_axis=0, tiled=True)  31 us
    all_to_all x1, blocking collectives, exchange(): return lax.all_to_all(blocks, axes, split_axis=0, concat_axis=0, tiled=True)  13.7 us
    pallas_call x1, Pallas kernels, layer(): pl.pallas_call(lambda *refs: layer_kernel(rows, parts, *refs), out_shape=...  12 us
    all_to_all x2, starting transfers between devices, exchange(): return lax.all_to_all(blocks, axes, split_axis=0, concat_axis=0, tiled=True)  10.3 us
  transfers between devices with their start and end apart: 3, of which 3 were waited for; matrix products, arithmetic and copies ran while one was open for 0% of the time, Pallas kernels for 1%

profile of v4, /device:TPU:1, one launch (start us, length us, event | category | flops | bytes accessed | tf_op | source)
XLA Modules:
  0.0 122.4 jit_solution(17351934813305193380)
XLA Ops:
  0.0 15.8 %conditional.2 = (bf16[24,1536]{1,0:T(8,128)(2,1)S(1)}, bf16[24,128]{1,0:T(8,128)(2,1)S(1)}, bf16[16,24,128]{2,1,0:T(8,128)(2,1)}, bf16[6,2,3072]{2,1,0:T(2,128)(2,1)}) conditional(s32[]{:T(128)} %convert_element_type.7, s32[6,2,8]{2,1,0:T(2,128)} %bitcast.33, (bf16[6,2,3072]{2,1,0:T(2,128)(2,1)}, s32[6,2,8]{2,1,0:T(2,128)}, ...), branch_computations={%region_0.0_spmd, %region_1.0_spmd} | conditional | flops 5082832896 | bytes 34945776 | solution.py:485
  0.0 0.7 tags.1
  0.7 13.7 %all_to_all.20.tags_ref = bf16[16,24,128]{2,1,0:T(8,128)(2,1)S(1)} all-to-all(bf16[16,24,128]{2,1,0:T(8,128)(2,1)S(1)} %get-tuple-element.54), channel_id=1, replica_groups=mesh['pp'=2,'ep'=16,'tp'=1] {'ep'}, dimensions={0} | all-to-all | bytes 196608 | tf_op jit(solution)/shard_map/cond/branch_0_fun/all_to_all | solution.py:24
  14.4 0.6 settle.1
  15.1 0.7 broadcast.7
  15.8 1.3 %collective-permute-start = (bf16[24,1536]{1,0:T(8,128)(2,1)S(1)}, bf16[24,1536]{1,0:T(8,128)(2,1)S(1)}, u32[]{:S(2)}, u32[]{:S(2)}) collective-permute-start(bf16[24,1536]{1,0:T(8,128)(2,1)S(1)} %get-tuple-element.90), channel_id=1, source_target_pairs={{0,16},{1,17},{2,18},{3,19},{4,20},{5,21},{6,22},{7,23},{8,24},{9,... | collective-permute-start | bytes 221192 | tf_op jit(solution)/shard_map/ppermute | solution.py:487
  17.0 49.2 %collective-permute-done = bf16[24,1536]{1,0:T(8,128)(2,1)S(1)} collective-permute-done((bf16[24,1536]{1,0:T(8,128)(2,1)S(1)}, bf16[24,1536]{1,0:T(8,128)(2,1)S(1)}, u32[]{:S(2)}, u32[]{:S(2)}) %collective-permute-start) | collective-permute-done | bytes 73760 | tf_op jit(solution)/shard_map/ppermute | solution.py:487
  66.2 56.2 %conditional.3 = (bf16[6,2,3072]{2,1,0:T(2,128)(2,1)}) conditional(s32[]{:T(128)} %convert_element_type.6, bf16[6,2,3072]{2,1,0:T(2,128)(2,1)} %get-tuple-element.89, (bf16[24,1536]{1,0:T(8,128)(2,1)S(1)}, bf16[1,3072]{1,0:T(2,128)(2,1)}, bf16[24,3072]{1,0:T(8,128)(2,1)}, bf16[16,24,128]{2,1,0:T(8,128)(2,1)}, bf16[3072,384]{1,0:T(8,128)(2,1)}, ...), branch_computations={%region_2.0_spmd, %region_3.0_spmd} | conditional | flops 5082832896 | bytes 35037936 | solution.py:488
  66.2 1.1 pack.3
  67.3 0.0 copy-start.1
  67.3 0.0 copy-start.2
  67.3 0.0 copy-start.4
  67.3 5.2 %all-to-all-start.3 = ((bf16[16,24,1536]{2,1,0:T(8,128)(2,1)}), bf16[16,24,1536]{2,1,0:T(8,128)(2,1)S(1)}, u32[]{:S(2)}, u32[]{:S(2)}) async-start(bf16[16,24,1536]{2,1,0:T(8,128)(2,1)} %pack.3), calls=%async_computation.3 | async-start | bytes 2359296 | tf_op jit(solution)/shard_map/cond/branch_1_fun/all_to_all | solution.py:24
  72.6 15.9 %all-to-all-done.3.refs_1_ = bf16[16,24,1536]{2,1,0:T(8,128)(2,1)S(1)} async-done(((bf16[16,24,1536]{2,1,0:T(8,128)(2,1)}), bf16[16,24,1536]{2,1,0:T(8,128)(2,1)S(1)}, u32[]{:S(2)}, u32[]{:S(2)}) %all-to-all-start.3) | async-done | bytes 1179680 | tf_op jit(solution)/shard_map/cond/branch_1_fun/all_to_all | solution.py:24
  88.5 0.0 copy-done.1
  88.5 0.0 copy-done.2
  88.5 0.0 copy-done.4
  88.5 12.0 %layer.3 = bf16[16,24,1536]{2,1,0:T(8,128)(2,1)} custom-call(s32[1]{0:T(128)} %bitcast.1.refs_0_, bf16[16,24,1536]{2,1,0:T(8,128)(2,1)S(1)} %all-to-all-done.3.refs_1_, bf16[1,3072]{1,0:T(2,128)(2,1)S(1)} %copy-done.4, bf16[24,3072]{1,0:T(8,128)(2,1)S(1)} %copy-done.1, bf16[16,24,128]{2,1,0:T(8,128)(2,1)S(1)} %copy-done.2, ...), custom_call_target="tpu_custom_call" | custom-call | flops 4982833152 | bytes 25952256 | tf_op jit(solution)/shard_map/cond/branch_1_fun/layer/pallas_call | solution.py:368
  100.5 5.1 %all-to-all-start.4 = ((bf16[16,24,1536]{2,1,0:T(8,128)(2,1)}), bf16[16,24,1536]{2,1,0:T(8,128)(2,1)S(1)}, u32[]{:S(2)}, u32[]{:S(2)}) async-start(bf16[16,24,1536]{2,1,0:T(8,128)(2,1)} %layer.3), calls=%async_computation.4 | async-start | bytes 2359296 | tf_op jit(solution)/shard_map/cond/branch_1_fun/all_to_all | solution.py:24
  105.6 0.8 base.3
  106.4 15.1 %all-to-all-done.4.refs_0_ = bf16[16,24,1536]{2,1,0:T(8,128)(2,1)S(1)} async-done(((bf16[16,24,1536]{2,1,0:T(8,128)(2,1)}), bf16[16,24,1536]{2,1,0:T(8,128)(2,1)S(1)}, u32[]{:S(2)}, u32[]{:S(2)}) %all-to-all-start.4) | async-done | bytes 1179680 | tf_op jit(solution)/shard_map/cond/branch_1_fun/all_to_all | solution.py:24
  121.5 0.9 combine.3
  (1 shorter events, 0.0 us)
Async XLA Ops:
  15.8 50.5 %collective-permute-start = (bf16[24,1536]{1,0:T(8,128)(2,1)S(1)}, bf16[24,1536]{1,0:T(8,128)(2,1)S(1)}, u32[]{:S(2)}, u32[]{:S(2)}) collective-permute-start(bf16[24,1536]{1,0:T(8,128)(2,1)S(1)} %get-tuple-element.90), channel_id=1, source_target_pairs={{0,16},{1,17},{2,18},{3,19},{4,20},{5,21},{6,22},{7,23},{8,24},{9,... | collective-permute-start | bytes 221192 | tf_op jit(solution)/shard_map/ppermute | solution.py:487
  67.3 21.1 %copy-start.1 = (bf16[24,3072]{1,0:T(8,128)(2,1)S(1)}, bf16[24,3072]{1,0:T(8,128)(2,1)}, u32[]{:S(2)}) copy-start(bf16[24,3072]{1,0:T(8,128)(2,1)} %get-tuple-element.74.refs_3_) | copy-start | bytes 442372 | tf_op jit(solution)/shard_map/cond
  67.3 21.1 %copy-start.2 = (bf16[16,24,128]{2,1,0:T(8,128)(2,1)S(1)}, bf16[16,24,128]{2,1,0:T(8,128)(2,1)}, u32[]{:S(2)}) copy-start(bf16[16,24,128]{2,1,0:T(8,128)(2,1)} %get-tuple-element.75.refs_4_) | copy-start | bytes 294916 | tf_op jit(solution)/shard_map/cond
  67.3 21.1 %copy-start.4 = (bf16[1,3072]{1,0:T(2,128)(2,1)S(1)}, bf16[1,3072]{1,0:T(2,128)(2,1)}, u32[]{:S(2)}) copy-start(bf16[1,3072]{1,0:T(2,128)(2,1)} %get-tuple-element.73.refs_2_) | copy-start | bytes 18436 | tf_op jit(solution)/shard_map/cond
  67.3 21.1 %all-to-all-start.3 = ((bf16[16,24,1536]{2,1,0:T(8,128)(2,1)}), bf16[16,24,1536]{2,1,0:T(8,128)(2,1)S(1)}, u32[]{:S(2)}, u32[]{:S(2)}) async-start(bf16[16,24,1536]{2,1,0:T(8,128)(2,1)} %pack.3), calls=%async_computation.3 | async-start | bytes 2359296 | tf_op jit(solution)/shard_map/cond/branch_1_fun/all_to_all | solution.py:24
  100.5 21.0 %all-to-all-start.4 = ((bf16[16,24,1536]{2,1,0:T(8,128)(2,1)}), bf16[16,24,1536]{2,1,0:T(8,128)(2,1)S(1)}, u32[]{:S(2)}, u32[]{:S(2)}) async-start(bf16[16,24,1536]{2,1,0:T(8,128)(2,1)} %layer.3), calls=%async_computation.4 | async-start | bytes 2359296 | tf_op jit(solution)/shard_map/cond/branch_1_fun/all_to_all | solution.py:24

commit v5 on v4

--- a/solution.py
+++ b/solution.py
@@ -14,7 +14,6 @@
 PIECE = 3 * MIB // 4
 HIDDEN = 256
 OUT = 512
-REFS = 21
 WHOLE = pl.BlockSpec(memory_space=pltpu.VMEM)
 SCALAR = pl.BlockSpec(memory_space=pltpu.SMEM)
 OUTSIDE = pl.BlockSpec(memory_space=pl.ANY)
@@ -150,10 +149,26 @@
             base_ref[rows, :] = pieces[p] + share * normed[p].astype(jnp.float32)
 
 
-def layer_kernel(rows, parts, place_ref, all_ref, gain_ref, router_ref, *refs):
-    tags_ref = None
-    if len(refs) > REFS:
+def head_kernel(gate_ref, up_ref, head_ref, sems):
+    size = head_ref.shape[1] // 2
+    cols = pl.ds(gate_ref.shape[1] - size, size)
+    copies = [
+        pltpu.make_async_copy(source.at[:, cols], head_ref.at[:, pl.ds(i * size, size)], sems.at[i])
+        for i, source in enumerate((gate_ref, up_ref))
+    ]
+    for copy in copies:
+        copy.start()
+    for copy in copies:
+        copy.wait()
+
+
+def layer_kernel(rows, parts, tagged, headed, place_ref, all_ref, gain_ref, router_ref, *refs):
+    tags_ref, head_ref = None, None
+    if not tagged:
         tags_ref, *refs = refs
+    if headed:
+        head_ref, *refs = refs
+    early = head_ref.shape[1] // 2 if headed else 0
     sources, out_ref = refs[:6], refs[6]
     held = refs[7:13]
     d_down, e_down = held[2], held[5]
@@ -171,7 +186,8 @@
     plan = []
     for which, hidden_ref in ((0, d_hidden), (3, e_hidden)):
         joined = hidden_ref.shape[1] % LANES == 0
-        for at, size in column_cuts(hidden_ref.shape[1], HIDDEN):
+        streamed = hidden_ref.shape[1] - (early if which == 0 else 0)
+        for at, size in column_cuts(streamed, HIDDEN):
             spots = (2 * at, 2 * at + size) if joined else (at, at)
             plan += [(which, at, spots[0], size), (which + 1, at, spots[1], size)]
     for at, size in out_cuts:
@@ -236,7 +252,13 @@
 
     def hidden(which, target):
         joined = target.shape[1] % LANES == 0
-        for at, size in column_cuts(target.shape[1], HIDDEN):
+        streamed = target.shape[1]
+        if which == 0 and headed:
+            streamed -= early
+            pair = jnp.dot(normed_ref[...], head_ref[...], preferred_element_type=jnp.float32)
+            gate_part, up_part = pair[:, :early], pair[:, early:]
+            target[:, streamed:] = (gate_part * sigmoid(gate_part) * up_part).astype(jnp.bfloat16)
+        for at, size in column_cuts(streamed, HIDDEN):
             arrive(which, at)
             arrive(which + 1, at)
             if joined:
@@ -364,12 +386,26 @@
     )(kept, tags, gain, router_t)
 
     n_dense, n_expert = weights[0].shape[1], weights[3].shape[1]
+    early = n_dense % HIDDEN if n_dense > HIDDEN and n_dense % LANES == 0 else 0
+    heads = []
+    if early:
+        head = pl.pallas_call(
+            head_kernel,
+            out_shape=pltpu.VMEM((width, 2 * early), jnp.bfloat16),
+            in_specs=[pl.BlockSpec(memory_space=pltpu.HBM)] * 2,
+            out_specs=WHOLE,
+            scratch_shapes=[pltpu.SemaphoreType.DMA((2,))],
+            compiler_params=pltpu.CompilerParams(vmem_limit_bytes=4 * MIB),
+            cost_estimate=pl.CostEstimate(flops=int(1e9), bytes_accessed=early * width * 4, transcendentals=0),
+            name="head",
+        )(*(pltpu.with_memory_space_constraint(w, pltpu.HBM) for w in weights[:2]))
+        heads = [pltpu.with_memory_space_constraint(head, pltpu.VMEM)]
     weights = [pltpu.with_memory_space_constraint(w, pltpu.HBM) for w in weights]
     partial = pl.pallas_call(
-        lambda *refs: layer_kernel(rows, parts, *refs),
-        out_shape=jax.ShapeDtypeStruct((n_groups, tall, span), jnp.bfloat16),
-        in_specs=[SCALAR] + [WHOLE] * (3 + len(all_tags)) + [pl.BlockSpec(memory_space=pltpu.HBM)] * 6,
-        out_specs=OUTSIDE,
+        lambda *refs: layer_kernel(rows, parts, known is None, early > 0, *refs),
+        out_shape=pltpu.HBM((n_groups, tall, span), jnp.bfloat16),
+        in_specs=[SCALAR] + [WHOLE] * (3 + len(all_tags) + len(heads)) + [pl.BlockSpec(memory_space=pltpu.HBM)] * 6,
+        out_specs=pl.BlockSpec(memory_space=pltpu.HBM),
         scratch_shapes=[
             *(pltpu.VMEM(shape, jnp.bfloat16) for shape in pair_shapes(width, n_dense)),
             pltpu.VMEM((n_dense, width), jnp.bfloat16),
@@ -391,7 +427,7 @@
             transcendentals=0,
         ),
         name="layer",
-    )(place.reshape(1).astype(jnp.int32), gathered, gain, router_t, *all_tags, *weights)
+    )(place.reshape(1).astype(jnp.int32), gathered, gain, router_t, *all_tags, *heads, *weights)
 
     share = tall // n_pairs
     received = exchange(partial.reshape(n_groups * n_pairs, share, span), ("ep", "tp"))

time: 123 us -> 121 us (0.984)
  waiting for transfers between devices: 80.2 us -> 78 us
    all_to_all x2, waiting for transfers between devices: 31 us -> 29.5 us  [exchange(): return lax.all_to_all(blocks, axes, split_axis=0, concat_axis=0, tiled=True)]
    pallas_call x1 -> x2, Pallas kernels: 12 us -> 13 us  [the longest x1 11.5 us: layer(): pl.pallas_call(lambda *refs: layer_kernel(rows, parts, known is None, ear...]
  transfers between devices with their start and end apart: 3 -> 3, of which waited for: 3 -> 3; matrix products, arithmetic and copies ran while one was open for 0% -> 0% of each run, Pallas kernels for 1% -> 2%
where the time goes in v5:
time: 121 us
  waiting for transfers between devices  78 us (64%)
  Pallas kernels  17.1 us (14%)
  blocking collectives  13.8 us (11%)
  starting transfers between devices  11.5 us (10%)
    ppermute x1, waiting for transfers between devices, on_device(): fed = lax.ppermute(folded, 'pp', [(phase - 1, phase)])  48.5 us
    all_to_all x2, waiting for transfers between devices, exchange(): return lax.all_to_all(blocks, axes, split_axis=0, concat_axis=0, tiled=True)  29.5 us
    all_to_all x1, blocking collectives, exchange(): return lax.all_to_all(blocks, axes, split_axis=0, concat_axis=0, tiled=True)  13.8 us
    pallas_call x1, Pallas kernels, layer(): pl.pallas_call(lambda *refs: layer_kernel(rows, parts, known is None, ear...  11.5 us
    all_to_all x2, starting transfers between devices, exchange(): return lax.all_to_all(blocks, axes, split_axis=0, concat_axis=0, tiled=True)  10.2 us
  transfers between devices with their start and end apart: 3, of which 3 were waited for; matrix products, arithmetic and copies ran while one was open for 0% of the time, Pallas kernels for 2%

profile of v5, /device:TPU:1, one launch (start us, length us, event | category | flops | bytes accessed | tf_op | source)
XLA Modules:
  0.0 121.1 jit_solution(11271126536636935310)
XLA Ops:
  0.0 15.8 %conditional.2 = (bf16[24,1536]{1,0:T(8,128)(2,1)S(1)}, bf16[24,128]{1,0:T(8,128)(2,1)S(1)}, bf16[16,24,128]{2,1,0:T(8,128)(2,1)}, bf16[6,2,3072]{2,1,0:T(2,128)(2,1)}) conditional(s32[]{:T(128)} %convert_element_type.7, s32[6,2,8]{2,1,0:T(2,128)} %bitcast.33, (bf16[6,2,3072]{2,1,0:T(2,128)(2,1)}, s32[6,2,8]{2,1,0:T(2,128)}, ...), branch_computations={%region_0.0_spmd, %region_1.0_spmd} | conditional | flops 6082833408 | bytes 36518640 | solution.py:521
  0.0 0.7 tags.1
  0.7 13.8 %all_to_all.20.tags_ref = bf16[16,24,128]{2,1,0:T(8,128)(2,1)S(1)} all-to-all(bf16[16,24,128]{2,1,0:T(8,128)(2,1)S(1)} %get-tuple-element.54), channel_id=1, replica_groups=mesh['pp'=2,'ep'=16,'tp'=1] {'ep'}, dimensions={0} | all-to-all | bytes 196608 | tf_op jit(solution)/shard_map/cond/branch_0_fun/all_to_all | solution.py:23
  14.5 0.6 settle.1
  15.1 0.7 broadcast.7
  15.8 1.3 %collective-permute-start = (bf16[24,1536]{1,0:T(8,128)(2,1)S(1)}, bf16[24,1536]{1,0:T(8,128)(2,1)S(1)}, u32[]{:S(2)}, u32[]{:S(2)}) collective-permute-start(bf16[24,1536]{1,0:T(8,128)(2,1)S(1)} %get-tuple-element.90), channel_id=1, source_target_pairs={{0,16},{1,17},{2,18},{3,19},{4,20},{5,21},{6,22},{7,23},{8,24},{9,... | collective-permute-start | bytes 221192 | tf_op jit(solution)/shard_map/ppermute | solution.py:523
  17.1 48.5 %collective-permute-done = bf16[24,1536]{1,0:T(8,128)(2,1)S(1)} collective-permute-done((bf16[24,1536]{1,0:T(8,128)(2,1)S(1)}, bf16[24,1536]{1,0:T(8,128)(2,1)S(1)}, u32[]{:S(2)}, u32[]{:S(2)}) %collective-permute-start) | collective-permute-done | bytes 73760 | tf_op jit(solution)/shard_map/ppermute | solution.py:523
  65.6 55.5 %conditional.3 = (bf16[6,2,3072]{2,1,0:T(2,128)(2,1)}) conditional(s32[]{:T(128)} %convert_element_type.6, bf16[6,2,3072]{2,1,0:T(2,128)(2,1)} %get-tuple-element.89, (bf16[24,1536]{1,0:T(8,128)(2,1)S(1)}, bf16[3072,384]{1,0:T(8,128)(2,1)}, bf16[3072,384]{1,0:T(8,128)(2,1)}, bf16[1,3072]{1,0:T(2,128)(2,1)}, bf16[24,3072]{1,0:T(8,128)(2,1)}, ...), branch_computations={%region_2.0_spmd, %region_3.0_spmd} | conditional | flops 6082833408 | bytes 36610800 | solution.py:524
  65.6 1.1 pack.3
  66.7 5.1 %all-to-all-start.3 = ((bf16[16,24,1536]{2,1,0:T(8,128)(2,1)}), bf16[16,24,1536]{2,1,0:T(8,128)(2,1)S(1)}, u32[]{:S(2)}, u32[]{:S(2)}) async-start(bf16[16,24,1536]{2,1,0:T(8,128)(2,1)} %pack.3), calls=%async_computation.3 | async-start | bytes 2359296 | tf_op jit(solution)/shard_map/cond/branch_1_fun/all_to_all | solution.py:23
  71.8 0.0 copy-start.1
  71.8 0.0 copy-start.2
  71.8 0.0 copy-start.4
  71.9 1.4 %head.3.refs_5_ = bf16[3072,256]{1,0:T(8,128)(2,1)S(1)} custom-call(bf16[3072,384]{1,0:T(8,128)(2,1)} %get-tuple-element.76.gate_ref.refs_6_, bf16[3072,384]{1,0:T(8,128)(2,1)} %get-tuple-element.77.up_ref.refs_7_), custom_call_target="tpu_custom_call" | custom-call | flops 1000000000 | bytes 1572864 | tf_op jit(solution)/shard_map/cond/branch_1_fun/head/pallas_call | solution.py:392
  73.3 14.4 %all-to-all-done.3.refs_1_ = bf16[16,24,1536]{2,1,0:T(8,128)(2,1)S(1)} async-done(((bf16[16,24,1536]{2,1,0:T(8,128)(2,1)}), bf16[16,24,1536]{2,1,0:T(8,128)(2,1)S(1)}, u32[]{:S(2)}, u32[]{:S(2)}) %all-to-all-start.3) | async-done | bytes 1179680 | tf_op jit(solution)/shard_map/cond/branch_1_fun/all_to_all | solution.py:23
  87.7 0.0 copy-done.1
  87.7 0.0 copy-done.2
  87.7 0.0 copy-done.4
  87.7 11.5 %layer.3 = bf16[16,24,1536]{2,1,0:T(8,128)(2,1)} custom-call(s32[1]{0:T(128)} %bitcast.1.refs_0_, bf16[16,24,1536]{2,1,0:T(8,128)(2,1)S(1)} %all-to-all-done.3.refs_1_, bf16[1,3072]{1,0:T(2,128)(2,1)S(1)} %copy-done.4, bf16[24,3072]{1,0:T(8,128)(2,1)S(1)} %copy-done.1, bf16[16,24,128]{2,1,0:T(8,128)(2,1)S(1)} %copy-done.2, ...), custom_call_target="tpu_custom_call" | custom-call | flops 4982833152 | bytes 25952256 | tf_op jit(solution)/shard_map/cond/branch_1_fun/layer/pallas_call | solution.py:404
  99.3 5.1 %all-to-all-start.4 = ((bf16[16,24,1536]{2,1,0:T(8,128)(2,1)}), bf16[16,24,1536]{2,1,0:T(8,128)(2,1)S(1)}, u32[]{:S(2)}, u32[]{:S(2)}) async-start(bf16[16,24,1536]{2,1,0:T(8,128)(2,1)} %layer.3), calls=%async_computation.4 | async-start | bytes 2359296 | tf_op jit(solution)/shard_map/cond/branch_1_fun/all_to_all | solution.py:23
  104.4 0.8 base.3
  105.1 15.1 %all-to-all-done.4.refs_0_ = bf16[16,24,1536]{2,1,0:T(8,128)(2,1)S(1)} async-done(((bf16[16,24,1536]{2,1,0:T(8,128)(2,1)}), bf16[16,24,1536]{2,1,0:T(8,128)(2,1)S(1)}, u32[]{:S(2)}, u32[]{:S(2)}) %all-to-all-start.4) | async-done | bytes 1179680 | tf_op jit(solution)/shard_map/cond/branch_1_fun/all_to_all | solution.py:23
  120.3 0.9 combine.3
  (1 shorter events, 0.0 us)
Async XLA Ops:
  15.8 49.8 %collective-permute-start = (bf16[24,1536]{1,0:T(8,128)(2,1)S(1)}, bf16[24,1536]{1,0:T(8,128)(2,1)S(1)}, u32[]{:S(2)}, u32[]{:S(2)}) collective-permute-start(bf16[24,1536]{1,0:T(8,128)(2,1)S(1)} %get-tuple-element.90), channel_id=1, source_target_pairs={{0,16},{1,17},{2,18},{3,19},{4,20},{5,21},{6,22},{7,23},{8,24},{9,... | collective-permute-start | bytes 221192 | tf_op jit(solution)/shard_map/ppermute | solution.py:523
  66.7 21.0 %all-to-all-start.3 = ((bf16[16,24,1536]{2,1,0:T(8,128)(2,1)}), bf16[16,24,1536]{2,1,0:T(8,128)(2,1)S(1)}, u32[]{:S(2)}, u32[]{:S(2)}) async-start(bf16[16,24,1536]{2,1,0:T(8,128)(2,1)} %pack.3), calls=%async_computation.3 | async-start | bytes 2359296 | tf_op jit(solution)/shard_map/cond/branch_1_fun/all_to_all | solution.py:23
  71.8 15.9 %copy-start.1 = (bf16[24,3072]{1,0:T(8,128)(2,1)S(1)}, bf16[24,3072]{1,0:T(8,128)(2,1)}, u32[]{:S(2)}) copy-start(bf16[24,3072]{1,0:T(8,128)(2,1)} %get-tuple-element.74.refs_3_) | copy-start | bytes 442372 | tf_op jit(solution)/shard_map/cond
  71.8 15.9 %copy-start.2 = (bf16[16,24,128]{2,1,0:T(8,128)(2,1)S(1)}, bf16[16,24,128]{2,1,0:T(8,128)(2,1)}, u32[]{:S(2)}) copy-start(bf16[16,24,128]{2,1,0:T(8,128)(2,1)} %get-tuple-element.75.refs_4_) | copy-start | bytes 294916 | tf_op jit(solution)/shard_map/cond
  71.8 15.9 %copy-start.4 = (bf16[1,3072]{1,0:T(2,128)(2,1)S(1)}, bf16[1,3072]{1,0:T(2,128)(2,1)}, u32[]{:S(2)}) copy-start(bf16[1,3072]{1,0:T(2,128)(2,1)} %get-tuple-element.73.refs_2_) | copy-start | bytes 18436 | tf_op jit(solution)/shard_map/cond
  99.3 21.0 %all-to-all-start.4 = ((bf16[16,24,1536]{2,1,0:T(8,128)(2,1)}), bf16[16,24,1536]{2,1,0:T(8,128)(2,1)S(1)}, u32[]{:S(2)}, u32[]{:S(2)}) async-start(bf16[16,24,1536]{2,1,0:T(8,128)(2,1)} %layer.3), calls=%async_computation.4 | async-start | bytes 2359296 | tf_op jit(solution)/shard_map/cond/branch_1_fun/all_to_all | solution.py:23

commit v6 on v5

--- a/solution.py
+++ b/solution.py
@@ -191,7 +191,7 @@
             spots = (2 * at, 2 * at + size) if joined else (at, at)
             plan += [(which, at, spots[0], size), (which + 1, at, spots[1], size)]
     for at, size in out_cuts:
-        plan += [(which, p * span + at, p * span + at, size) for which in (2, 5) for p in range(parts)]
+        plan += [(which, p * span + at, p * span + at, size) for p in range(parts) for which in (2, 5)]
     held = tuple(
         held[i - 1] if i in (1, 4) and refs_joined(held[i - 1], sources[i]) else h for i, h in enumerate(held)
     )

time: 121 us -> 121 us (level)
  no operation moved by 1% of the time
where the time goes in v6:
time: 121 us
  waiting for transfers between devices  78 us (64%)
  Pallas kernels  17.1 us (14%)
  blocking collectives  13.8 us (11%)
  starting transfers between devices  11.5 us (10%)
    ppermute x1, waiting for transfers between devices, on_device(): fed = lax.ppermute(folded, 'pp', [(phase - 1, phase)])  48.5 us
    all_to_all x2, waiting for transfers between devices, exchange(): return lax.all_to_all(blocks, axes, split_axis=0, concat_axis=0, tiled=True)  29.5 us
    all_to_all x1, blocking collectives, exchange(): return lax.all_to_all(blocks, axes, split_axis=0, concat_axis=0, tiled=True)  13.8 us
    pallas_call x1, Pallas kernels, layer(): pl.pallas_call(lambda *refs: layer_kernel(rows, parts, known is None, ear...  11.5 us
    all_to_all x2, starting transfers between devices, exchange(): return lax.all_to_all(blocks, axes, split_axis=0, concat_axis=0, tiled=True)  10.2 us
  transfers between devices with their start and end apart: 3, of which 3 were waited for; matrix products, arithmetic and copies ran while one was open for 0% of the time, Pallas kernels for 2%

profile of v6, /device:TPU:1, one launch (start us, length us, event | category | flops | bytes accessed | tf_op | source)
XLA Modules:
  0.0 121.1 jit_solution(9545937930015781977)
XLA Ops:
  0.0 15.8 %conditional.2 = (bf16[24,1536]{1,0:T(8,128)(2,1)S(1)}, bf16[24,128]{1,0:T(8,128)(2,1)S(1)}, bf16[16,24,128]{2,1,0:T(8,128)(2,1)}, bf16[6,2,3072]{2,1,0:T(2,128)(2,1)}) conditional(s32[]{:T(128)} %convert_element_type.7, s32[6,2,8]{2,1,0:T(2,128)} %bitcast.33, (bf16[6,2,3072]{2,1,0:T(2,128)(2,1)}, s32[6,2,8]{2,1,0:T(2,128)}, ...), branch_computations={%region_0.0_spmd, %region_1.0_spmd} | conditional | flops 6082833408 | bytes 36518640 | solution.py:521
  0.0 0.7 tags.1
  0.7 13.8 %all_to_all.20.tags_ref = bf16[16,24,128]{2,1,0:T(8,128)(2,1)S(1)} all-to-all(bf16[16,24,128]{2,1,0:T(8,128)(2,1)S(1)} %get-tuple-element.54), channel_id=1, replica_groups=mesh['pp'=2,'ep'=16,'tp'=1] {'ep'}, dimensions={0} | all-to-all | bytes 196608 | tf_op jit(solution)/shard_map/cond/branch_0_fun/all_to_all | solution.py:23
  14.5 0.6 settle.1
  15.1 0.7 broadcast.7
  15.8 1.3 %collective-permute-start = (bf16[24,1536]{1,0:T(8,128)(2,1)S(1)}, bf16[24,1536]{1,0:T(8,128)(2,1)S(1)}, u32[]{:S(2)}, u32[]{:S(2)}) collective-permute-start(bf16[24,1536]{1,0:T(8,128)(2,1)S(1)} %get-tuple-element.90), channel_id=1, source_target_pairs={{0,16},{1,17},{2,18},{3,19},{4,20},{5,21},{6,22},{7,23},{8,24},{9,... | collective-permute-start | bytes 221192 | tf_op jit(solution)/shard_map/ppermute | solution.py:523
  17.1 48.5 %collective-permute-done = bf16[24,1536]{1,0:T(8,128)(2,1)S(1)} collective-permute-done((bf16[24,1536]{1,0:T(8,128)(2,1)S(1)}, bf16[24,1536]{1,0:T(8,128)(2,1)S(1)}, u32[]{:S(2)}, u32[]{:S(2)}) %collective-permute-start) | collective-permute-done | bytes 73760 | tf_op jit(solution)/shard_map/ppermute | solution.py:523
  65.6 55.5 %conditional.3 = (bf16[6,2,3072]{2,1,0:T(2,128)(2,1)}) conditional(s32[]{:T(128)} %convert_element_type.6, bf16[6,2,3072]{2,1,0:T(2,128)(2,1)} %get-tuple-element.89, (bf16[24,1536]{1,0:T(8,128)(2,1)S(1)}, bf16[3072,384]{1,0:T(8,128)(2,1)}, bf16[3072,384]{1,0:T(8,128)(2,1)}, bf16[1,3072]{1,0:T(2,128)(2,1)}, bf16[24,3072]{1,0:T(8,128)(2,1)}, ...), branch_computations={%region_2.0_spmd, %region_3.0_spmd} | conditional | flops 6082833408 | bytes 36610800 | solution.py:524
  65.6 1.1 pack.3
  66.7 5.1 %all-to-all-start.3 = ((bf16[16,24,1536]{2,1,0:T(8,128)(2,1)}), bf16[16,24,1536]{2,1,0:T(8,128)(2,1)S(1)}, u32[]{:S(2)}, u32[]{:S(2)}) async-start(bf16[16,24,1536]{2,1,0:T(8,128)(2,1)} %pack.3), calls=%async_computation.3 | async-start | bytes 2359296 | tf_op jit(solution)/shard_map/cond/branch_1_fun/all_to_all | solution.py:23
  71.8 0.0 copy-start.1
  71.8 0.0 copy-start.2
  71.8 0.0 copy-start.4
  71.9 1.4 %head.3.refs_5_ = bf16[3072,256]{1,0:T(8,128)(2,1)S(1)} custom-call(bf16[3072,384]{1,0:T(8,128)(2,1)} %get-tuple-element.76.gate_ref.refs_6_, bf16[3072,384]{1,0:T(8,128)(2,1)} %get-tuple-element.77.up_ref.refs_7_), custom_call_target="tpu_custom_call" | custom-call | flops 1000000000 | bytes 1572864 | tf_op jit(solution)/shard_map/cond/branch_1_fun/head/pallas_call | solution.py:392
  73.3 14.4 %all-to-all-done.3.refs_1_ = bf16[16,24,1536]{2,1,0:T(8,128)(2,1)S(1)} async-done(((bf16[16,24,1536]{2,1,0:T(8,128)(2,1)}), bf16[16,24,1536]{2,1,0:T(8,128)(2,1)S(1)}, u32[]{:S(2)}, u32[]{:S(2)}) %all-to-all-start.3) | async-done | bytes 1179680 | tf_op jit(solution)/shard_map/cond/branch_1_fun/all_to_all | solution.py:23
  87.7 0.0 copy-done.1
  87.7 0.0 copy-done.2
  87.7 0.0 copy-done.4
  87.7 11.5 %layer.3 = bf16[16,24,1536]{2,1,0:T(8,128)(2,1)} custom-call(s32[1]{0:T(128)} %bitcast.1.refs_0_, bf16[16,24,1536]{2,1,0:T(8,128)(2,1)S(1)} %all-to-all-done.3.refs_1_, bf16[1,3072]{1,0:T(2,128)(2,1)S(1)} %copy-done.4, bf16[24,3072]{1,0:T(8,128)(2,1)S(1)} %copy-done.1, bf16[16,24,128]{2,1,0:T(8,128)(2,1)S(1)} %copy-done.2, ...), custom_call_target="tpu_custom_call" | custom-call | flops 4982833152 | bytes 25952256 | tf_op jit(solution)/shard_map/cond/branch_1_fun/layer/pallas_call | solution.py:404
  99.3 5.1 %all-to-all-start.4 = ((bf16[16,24,1536]{2,1,0:T(8,128)(2,1)}), bf16[16,24,1536]{2,1,0:T(8,128)(2,1)S(1)}, u32[]{:S(2)}, u32[]{:S(2)}) async-start(bf16[16,24,1536]{2,1,0:T(8,128)(2,1)} %layer.3), calls=%async_computation.4 | async-start | bytes 2359296 | tf_op jit(solution)/shard_map/cond/branch_1_fun/all_to_all | solution.py:23
  104.4 0.8 base.3
  105.1 15.1 %all-to-all-done.4.refs_0_ = bf16[16,24,1536]{2,1,0:T(8,128)(2,1)S(1)} async-done(((bf16[16,24,1536]{2,1,0:T(8,128)(2,1)}), bf16[16,24,1536]{2,1,0:T(8,128)(2,1)S(1)}, u32[]{:S(2)}, u32[]{:S(2)}) %all-to-all-start.4) | async-done | bytes 1179680 | tf_op jit(solution)/shard_map/cond/branch_1_fun/all_to_all | solution.py:23
  120.3 0.9 combine.3
  (1 shorter events, 0.0 us)
Async XLA Ops:
  15.8 49.8 %collective-permute-start = (bf16[24,1536]{1,0:T(8,128)(2,1)S(1)}, bf16[24,1536]{1,0:T(8,128)(2,1)S(1)}, u32[]{:S(2)}, u32[]{:S(2)}) collective-permute-start(bf16[24,1536]{1,0:T(8,128)(2,1)S(1)} %get-tuple-element.90), channel_id=1, source_target_pairs={{0,16},{1,17},{2,18},{3,19},{4,20},{5,21},{6,22},{7,23},{8,24},{9,... | collective-permute-start | bytes 221192 | tf_op jit(solution)/shard_map/ppermute | solution.py:523
  66.7 21.0 %all-to-all-start.3 = ((bf16[16,24,1536]{2,1,0:T(8,128)(2,1)}), bf16[16,24,1536]{2,1,0:T(8,128)(2,1)S(1)}, u32[]{:S(2)}, u32[]{:S(2)}) async-start(bf16[16,24,1536]{2,1,0:T(8,128)(2,1)} %pack.3), calls=%async_computation.3 | async-start | bytes 2359296 | tf_op jit(solution)/shard_map/cond/branch_1_fun/all_to_all | solution.py:23
  71.8 15.9 %copy-start.1 = (bf16[24,3072]{1,0:T(8,128)(2,1)S(1)}, bf16[24,3072]{1,0:T(8,128)(2,1)}, u32[]{:S(2)}) copy-start(bf16[24,3072]{1,0:T(8,128)(2,1)} %get-tuple-element.74.refs_3_) | copy-start | bytes 442372 | tf_op jit(solution)/shard_map/cond
  71.8 15.9 %copy-start.2 = (bf16[16,24,128]{2,1,0:T(8,128)(2,1)S(1)}, bf16[16,24,128]{2,1,0:T(8,128)(2,1)}, u32[]{:S(2)}) copy-start(bf16[16,24,128]{2,1,0:T(8,128)(2,1)} %get-tuple-element.75.refs_4_) | copy-start | bytes 294916 | tf_op jit(solution)/shard_map/cond
  71.8 15.9 %copy-start.4 = (bf16[1,3072]{1,0:T(2,128)(2,1)S(1)}, bf16[1,3072]{1,0:T(2,128)(2,1)}, u32[]{:S(2)}) copy-start(bf16[1,3072]{1,0:T(2,128)(2,1)} %get-tuple-element.73.refs_2_) | copy-start | bytes 18436 | tf_op jit(solution)/shard_map/cond
  99.3 21.0 %all-to-all-start.4 = ((bf16[16,24,1536]{2,1,0:T(8,128)(2,1)}), bf16[16,24,1536]{2,1,0:T(8,128)(2,1)S(1)}, u32[]{:S(2)}, u32[]{:S(2)}) async-start(bf16[16,24,1536]{2,1,0:T(8,128)(2,1)} %layer.3), calls=%async_computation.4 | async-start | bytes 2359296 | tf_op jit(solution)/shard_map/cond/branch_1_fun/all_to_all | solution.py:23
